TPU v7x, 32 devices: a whole 2x2x4 slice. The times are simulated.
32 devices in a mesh: radial: 8 (over z, x), phi: 4 (over y, core).
Axes of the slice: x: 2, y: 2, z: 4, core: 2. Of those that a mesh axis runs over, the one named last changes fastest.
Arguments:
- conserved: float32 [8, 64, 64, 128], P(None, 'radial', 'phi'), may hold values from -2.5 to 7, as said below
- core_mass: float32 [1], replicated, may hold values from 0.2 to 1
Outputs:
- advanced: float32 [8, 64, 64, 128], P(None, 'radial', 'phi')
- enclosed_mass: float32 [64], P('radial')
Inputs may be any that keep to these rules, and one draw needn't show every extreme that they name: conserved[0] (density) lies between 0.4 and 2.5; conserved[4] exceeds (conserved[1]^2 + conserved[2]^2 + conserved[3]^2)/(2 conserved[0]) by at least 0.6; the speeds |conserved[m]/conserved[0]| stay below 1; conserved[5..7] lie between 0 and conserved[0].
All inputs are finite; a program needn't handle non-finite values.
Results may differ from a plain program's by a relative error of at most 0.0003.
Values sent between devices are 32-bit elements; how exact they have to be, the bound alone decides.
A program may use at most 64 MiB of HBM per device.

v0:
```python
import functools
import math

import jax
import jax.numpy as jnp
import numpy as np
from jax import lax
from jax.experimental import pallas as pl
from jax.experimental.pallas import tpu as pltpu
from jax.sharding import PartitionSpec as P

ADIABATIC = 4.0 / 3.0
INNER_RADIUS = 1.0
OUTER_RADIUS = 2.0
COURANT = 0.4
GRAVITY_KICK = 0.004
MINIMUM_DENSITY = 0.05
PRESSURE_FLOOR = 0.01
MESH = pl.DeviceIdType.MESH
TILE = 8
PAD = 8


def step_sizes(radial_total, phi_total, theta_total):
    theta_step = math.pi / theta_total
    phi_step = 2.0 * math.pi / phi_total
    polar_width = INNER_RADIUS * math.sin(0.5 * theta_step) * phi_step
    radial_step = min(2.0 * polar_width, (OUTER_RADIUS - INNER_RADIUS) / radial_total)
    timestep = COURANT * min(radial_step, polar_width)
    return (radial_step, theta_step, phi_step, timestep)


def angle_tables(theta_cells, theta_step):
    step = np.float32(theta_step)
    centre = (np.arange(theta_cells, dtype=np.float32) + np.float32(0.5)) * step
    face = np.arange(theta_cells + 1, dtype=np.float32) * step
    sine = np.sin(centre.astype(np.float64))
    cosine = np.cos(centre.astype(np.float64))
    face_sine = np.sin(face.astype(np.float64))
    zero = np.zeros(theta_cells)
    rows = [sine, face_sine[:-1], face_sine[1:], cosine / sine, 1.0 / sine, zero, zero, zero]
    return np.stack(rows).astype(np.float32)


def half_slope(below, above):
    return 0.5 * (
        jnp.maximum(jnp.minimum(below, above), 0.0) + jnp.minimum(jnp.maximum(below, above), 0.0)
    )


def thermo(q):
    density = jnp.maximum(q[0], MINIMUM_DENSITY)
    inverse = 1.0 / density
    kinetic = 0.5 * (q[1] * q[1] + q[2] * q[2] + q[3] * q[3]) * inverse
    pressure = jnp.maximum((ADIABATIC - 1.0) * (q[4] - kinetic), PRESSURE_FLOOR * density)
    return density, inverse, pressure


def physical(q, component):
    _, inverse, pressure = thermo(q)
    normal = q[component] * inverse
    squared = ADIABATIC * pressure * inverse
    return normal, pressure, jnp.abs(normal) + squared * lax.rsqrt(squared)


def flux(left, right, component):
    left_v, left_p, left_a = physical(left, component)
    right_v, right_p, right_a = physical(right, component)
    signal = jnp.maximum(left_a, right_a)
    left_w = 0.5 * (left_v + signal)
    right_w = 0.5 * (right_v - signal)
    out = [a * left_w + b * right_w for a, b in zip(left, right)]
    out[component] = out[component] + 0.5 * (left_p + right_p)
    out[4] = out[4] + 0.5 * (left_p * left_v + right_p * right_v)
    return out


def two_faces(rows, component):
    lower_left, lower_right, upper_left, upper_right = [], [], [], []
    for a, b, c, d, e in zip(*rows):
        ab, bc, cd, de = b - a, c - b, d - c, e - d
        sb, sc, sd = half_slope(ab, bc), half_slope(bc, cd), half_slope(cd, de)
        lower_left.append(b + sb)
        lower_right.append(c - sc)
        upper_left.append(c + sc)
        upper_right.append(d - sd)
    return flux(lower_left, lower_right, component), flux(upper_left, upper_right, component)


def kernel(
    sizes,
    counts,
    core_ref,
    table_ref,
    input_ref,
    out_ref,
    mass_ref,
    first,
    second,
    edge,
    halo,
    part,
    slab_part,
    got,
    pull,
    table,
    core,
    load_sem,
    radial_send,
    radial_recv,
    phi_send,
    phi_recv,
    part_send,
    part_recv,
):
    radial_step, theta_step, phi_step, timestep = sizes
    slabs, wedges = counts
    variables, rows, cells, lanes = input_ref.shape
    tiles = cells // TILE
    strength = GRAVITY_KICK / timestep
    slab, wedge = lax.axis_index("radial"), lax.axis_index("phi")
    has_up, has_down = slab < slabs - 1, slab > 0

    load = pltpu.make_async_copy(
        input_ref, first.at[:, pl.ds(2, rows), pl.ds(PAD, cells), :], load_sem.at[0]
    )
    load.start()
    load_table = pltpu.make_async_copy(table_ref, table, load_sem.at[1])
    load_table.start()
    load_core = pltpu.make_async_copy(core_ref, core, load_sem.at[2])
    load_core.start()

    def radial_peer(jump):
        return (lax.rem(slab + jump, slabs), wedge)

    def phi_peer(jump):
        return (slab, lax.rem(wedge + jump, wedges))

    barrier = pltpu.get_barrier_semaphore()
    jumps = [(i, 0) for i in range(1, slabs)] + [(0, j) for j in range(1, wedges)]

    def peer_at(jump):
        return (radial_peer(jump[0])[0], phi_peer(jump[1])[1])

    for jump in jumps:
        pl.semaphore_signal(barrier, inc=1, device_id=peer_at(jump), device_id_type=MESH)
    load.wait()
    load_table.wait()
    load_core.wait()

    def remote(src, dst, send, recv, peer):
        return pltpu.make_async_remote_copy(
            src_ref=src, dst_ref=dst, send_sem=send, recv_sem=recv, device_id=peer,
            device_id_type=MESH,
        )

    def radial_copies(buffer, section, tile):
        where = pl.ds(PAD + TILE * tile, TILE)
        slot = (section * tiles + tile) * 2
        up = remote(
            buffer.at[:, pl.ds(rows, 2), where, :], buffer.at[:, pl.ds(0, 2), where, :],
            radial_send.at[slot], radial_recv.at[slot], radial_peer(1),
        )
        down = remote(
            buffer.at[:, pl.ds(2, 2), where, :], buffer.at[:, pl.ds(rows + 2, 2), where, :],
            radial_send.at[slot + 1], radial_recv.at[slot + 1], radial_peer(slabs - 1),
        )
        return up, down

    def radial_start(copies):
        up, down = copies

        @pl.when(has_up)
        def _():
            up.start()

        @pl.when(has_down)
        def _():
            down.start()

    def radial_sent(copies):
        up, down = copies

        @pl.when(has_up)
        def _():
            up.wait_send()

        @pl.when(has_down)
        def _():
            down.wait_send()

    def radial_land(copies, buffer, tile):
        up, down = copies
        where = pl.ds(PAD + TILE * tile, TILE)

        @pl.when(has_down)
        def _():
            up.wait_recv()

        @pl.when(jnp.logical_not(has_down))
        def _():
            value = buffer[:, 2, where, :]
            buffer[:, 0, where, :] = value
            buffer[:, 1, where, :] = value

        @pl.when(has_up)
        def _():
            down.wait_recv()

        @pl.when(jnp.logical_not(has_up))
        def _():
            value = buffer[:, rows + 1, where, :]
            buffer[:, rows + 2, where, :] = value
            buffer[:, rows + 3, where, :] = value

    whole, inside, low_edge, high_edge = (0, rows), (2, rows - 4), (0, 2), (rows - 2, 2)

    def phi_copies(section, piece, slot):
        where = pl.ds(*piece)
        return [
            remote(
                edge.at[section * 2 + side, :, where], halo.at[section * 2 + side, :, where],
                phi_send.at[slot + side], phi_recv.at[slot + side], phi_peer(jump),
            )
            for side, jump in ((0, wedges - 1), (1, 1))
        ]

    def phi_pack(buffer, section, side, piece):
        begin, count = piece
        start = PAD if side == 0 else PAD + cells - 2
        edge[section * 2 + side, :, pl.ds(begin, count)] = buffer[
            :, pl.ds(2 + begin, count), pl.ds(start, 2), :
        ]

    def phi_unpack(buffer, section, side, piece):
        begin, count = piece
        start = PAD + cells if side == 0 else PAD - 2
        buffer[:, pl.ds(2 + begin, count), pl.ds(start, 2), :] = halo[
            section * 2 + side, :, pl.ds(begin, count)
        ]

    shape = (TILE, lanes)
    lane = lax.broadcasted_iota(jnp.int32, (rows, lanes), 1)
    line = lax.broadcasted_iota(jnp.int32, (rows, lanes), 0)
    column = jnp.sum(first[0, pl.ds(2, rows), pl.ds(PAD, cells), :], axis=1)
    column = jnp.sum(column * table[0:1, :], axis=1, keepdims=True)
    centres = INNER_RADIUS + (
        (slab * rows + line).astype(jnp.float32) + 0.5
    ) * radial_step
    column = column * centres * centres * (radial_step * theta_step * phi_step)
    part[...] = jnp.sum(jnp.where(lane == line, column, 0.0), axis=0, keepdims=True)
    got[0] = part[...]
    phi_pack(first, 0, 0, whole)
    phi_pack(first, 0, 1, whole)
    pl.semaphore_wait(barrier, len(jumps))

    def wedge_sum():
        shells = jnp.zeros((1, lanes), jnp.float32)
        for w in range(wedges):
            shells = shells + got[lax.rem(wedge + wedges - w, wedges)]
        return shells

    part_copies = []
    for j in range(1, wedges):
        i, slot = 0, j
        part_copies.append(
            remote(part, got.at[slot], part_send.at[slot], part_recv.at[slot], peer_at((i, j)))
        )
    first_radial = [radial_copies(first, 0, t) for t in range(tiles)]
    second_radial = [radial_copies(second, 1, t) for t in range(tiles)]
    first_phi = phi_copies(0, whole, 0)
    inside_phi = phi_copies(1, inside, 2)
    low_phi, high_phi = phi_copies(1, low_edge, 4), phi_copies(1, high_edge, 6)
    for copy in part_copies + first_phi:
        copy.start()
    radial_start(first_radial[0])
    for copy in part_copies:
        copy.wait_recv()
    slab_part[...] = wedge_sum()
    slab_copies = []
    for j in range(1, slabs):
        slot = j * wedges
        slab_copies.append(
            remote(
                slab_part, got.at[slot], part_send.at[slot], part_recv.at[slot], radial_peer(j)
            )
        )
    for copy in slab_copies:
        copy.start()
    for t in range(1, tiles):
        radial_start(first_radial[t])

    lane_tile = lax.broadcasted_iota(jnp.int32, shape, 1)
    is_first, is_last = lane_tile == 0, lane_tile == lanes - 1

    def rate(buffer, r, tile, radial=True, rest=True):
        start = PAD + TILE * tile

        def at(row, offset):
            return [buffer[k, row + 2, pl.ds(start + offset, TILE), :] for k in range(variables)]

        def spread(value):
            return jnp.broadcast_to(value, shape)

        index = jnp.full(shape, slab * rows + r, jnp.int32).astype(jnp.float32)
        radius = INNER_RADIUS + (index + 0.5) * radial_step
        inner, outer = radius - 0.5 * radial_step, radius + 0.5 * radial_step
        inverse_r = 1.0 / radius
        centre = at(r, 0)
        total = [0.0] * variables
        if radial:
            lower, upper = two_faces([at(r + o, 0) if o else centre for o in range(-2, 3)], 1)
            scale = inverse_r * inverse_r * (1.0 / radial_step)
            area_in, area_out = inner * inner * scale, outer * outer * scale
            total = [area_in * a - area_out * b for a, b in zip(lower, upper)]
        if not rest:
            return total
        lower, upper = two_faces([at(r, o) if o else centre for o in range(-2, 3)], 3)
        around = inverse_r * spread(table[4:5, :])
        scale = around * (1.0 / phi_step)
        total = [t + (a - b) * scale for t, a, b in zip(total, lower, upper)]
        left, right = [], []
        for q in centre:
            after = jnp.where(is_last, q, pltpu.roll(q, lanes - 1, 1))
            above = after - q
            below = jnp.where(is_first, 0.0, pltpu.roll(above, 1, 1))
            slope = half_slope(below, above)
            left.append(q + slope)
            right.append(jnp.where(is_last, q, pltpu.roll(q - slope, lanes - 1, 1)))
        upper = flux(left, right, 2)
        scale = around * (1.0 / theta_step)
        low_sine, high_sine = spread(table[1:2, :]), spread(table[2:3, :])
        low_area, high_area = low_sine * scale, high_sine * scale
        total = [
            t + (low_area * pltpu.roll(f, 1, 1) - high_area * f) for t, f in zip(total, upper)
        ]
        density, inverse, pressure = thermo(centre)
        vr, vt, vp = (centre[m] * inverse for m in (1, 2, 3))
        cot = spread(table[3:4, :])
        total[1] = total[1] + (2.0 * pressure + density * (vt * vt + vp * vp)) * inverse_r
        total[2] = total[2] + (
            (pressure + density * vp * vp) * cot - density * vr * vt
        ) * inverse_r
        total[3] = total[3] - density * vp * (vr + vt * cot) * inverse_r
        return centre, density, total

    def gravity_at(r):
        return jnp.broadcast_to(pull[pl.ds(r, 1), :], shape)

    def with_gravity(rates, r):
        centre, density, total = rates
        gravity = gravity_at(r)
        total[1] = total[1] - density * gravity
        total[4] = total[4] - centre[1] * gravity
        return centre, total

    def section_one(r, tile):
        centre, _, total = rate(first, r, tile)
        where = pl.ds(PAD + TILE * tile, TILE)
        for k in range(variables):
            second[k, r + 2, where, :] = centre[k] + timestep * total[k]

    def rest_one(r, tile):
        centre, _, total = rate(first, r, tile, radial=False)
        where = pl.ds(PAD + TILE * tile, TILE)
        for k in range(variables):
            second[k, r + 2, where, :] = centre[k] + timestep * total[k]

    def radial_one(r, tile):
        total = rate(first, r, tile, rest=False)
        where = pl.ds(PAD + TILE * tile, TILE)
        for k in range(variables):
            second[k, r + 2, where, :] = second[k, r + 2, where, :] + timestep * total[k]

    def late_gravity(r, tile):
        where = pl.ds(PAD + TILE * tile, TILE)
        gravity = timestep * gravity_at(r)
        density = jnp.maximum(first[0, r + 2, where, :], MINIMUM_DENSITY)
        second[1, r + 2, where, :] = second[1, r + 2, where, :] - density * gravity
        second[4, r + 2, where, :] = (
            second[4, r + 2, where, :] - first[1, r + 2, where, :] * gravity
        )

    def section_two(r, tile, radial=True):
        centre, total = with_gravity(rate(second, r, tile, radial=radial), r)
        where = pl.ds(PAD + TILE * tile, TILE)
        into = pl.ds(TILE * tile, TILE)
        for k in range(variables):
            begin = first[k, r + 2, where, :]
            out_ref[k, r, into, :] = 0.5 * begin + 0.5 * (centre[k] + timestep * total[k])

    def radial_two(r, tile):
        total = rate(second, r, tile, rest=False)
        into = pl.ds(TILE * tile, TILE)
        for k in range(variables):
            out_ref[k, r, into, :] = out_ref[k, r, into, :] + (0.5 * timestep) * total[k]

    def each_row(low, high, step):
        lax.fori_loop(low, high, lambda r, _: (step(r), 0)[1], 0)

    def each_edge(step):
        lax.fori_loop(
            0, 4, lambda i, _: (step(i + (i // 2) * (rows - 4)), 0)[1], 0
        )

    def all_tiles(step):
        def run(r):
            for t in range(tiles):
                step(r, t)

        return run

    for side, copy in enumerate(first_phi):
        copy.wait_recv()
        phi_unpack(first, 0, side, whole)
    each_row(2, rows - 2, all_tiles(section_one))
    each_edge(all_tiles(rest_one))
    radial_land(first_radial[0], first, 0)
    each_edge(lambda r: radial_one(r, 0))

    for copy in slab_copies:
        copy.wait_recv()
    before = jnp.zeros((1, lanes), jnp.float32)
    for j in range(slabs - 1, 0, -1):
        before = before + jnp.where(slab >= j, got[j * wedges], 0.0)
    before = jnp.sum(before, axis=1, keepdims=True)
    weight = jnp.where(lane < line, 1.0, jnp.where(lane == line, 0.5, 0.0))
    within = jnp.sum(weight * slab_part[...], axis=1, keepdims=True)
    enclosed = core[0] + before + within + jnp.zeros((rows, lanes), jnp.float32)
    mass_ref[...] = jnp.sum(jnp.where(lane == line, enclosed, 0.0), axis=0, keepdims=True)[:, :rows]
    pull[...] = strength * enclosed / (centres * centres)
    for t in range(tiles):
        if t:
            radial_land(first_radial[t], first, t)
            each_edge(lambda r: radial_one(r, t))
        each_edge(lambda r: late_gravity(r, t))
        radial_start(second_radial[t])
        for side, last in ((0, 0), (1, tiles - 1)):
            if t == last:
                phi_pack(second, 1, side, low_edge)
                phi_pack(second, 1, side, high_edge)
                low_phi[side].start()
                high_phi[side].start()
        if t == 0:
            each_row(2, rows - 2, all_tiles(late_gravity))
            for side, copy in enumerate(inside_phi):
                phi_pack(second, 1, side, inside)
                copy.start()
    for side, copy in enumerate(inside_phi):
        copy.wait_recv()
        phi_unpack(second, 1, side, inside)
    each_row(2, rows - 2, all_tiles(section_two))
    for side in range(2):
        low_phi[side].wait_recv()
        high_phi[side].wait_recv()
        phi_unpack(second, 1, side, low_edge)
        phi_unpack(second, 1, side, high_edge)
    each_edge(all_tiles(lambda r, t: section_two(r, t, False)))
    for t in range(tiles):
        radial_land(second_radial[t], second, t)
        each_edge(lambda r: radial_two(r, t))

    for copy in part_copies + slab_copies + first_phi + inside_phi + low_phi + high_phi:
        copy.wait_send()
    for copies in first_radial + second_radial:
        radial_sent(copies)


def body(conserved, core_mass):
    variables, rows, cells, lanes = conserved.shape
    slabs, wedges = lax.axis_size("radial"), lax.axis_size("phi")
    sizes = step_sizes(rows * slabs, cells * wedges, lanes)
    table = jnp.asarray(angle_tables(lanes, sizes[1]))
    tiles = cells // TILE
    padded = (variables, rows + 4, cells + 2 * PAD, lanes)
    vmem = pl.BlockSpec(memory_space=pltpu.VMEM)
    dma = pltpu.SemaphoreType.DMA
    advanced, mass = pl.pallas_call(
        functools.partial(kernel, sizes, (slabs, wedges)),
        out_shape=(
            pltpu.VMEM(conserved.shape, jnp.float32),
            pltpu.VMEM((1, rows), jnp.float32),
        ),
        in_specs=[pl.BlockSpec(memory_space=pl.ANY)] * 3,
        out_specs=(vmem, vmem),
        scratch_shapes=[
            pltpu.VMEM(padded, jnp.float32),
            pltpu.VMEM(padded, jnp.float32),
            pltpu.VMEM((4, variables, rows, 2, lanes), jnp.float32),
            pltpu.VMEM((4, variables, rows, 2, lanes), jnp.float32),
            pltpu.VMEM((1, lanes), jnp.float32),
            pltpu.VMEM((1, lanes), jnp.float32),
            pltpu.VMEM((slabs * wedges, 1, lanes), jnp.float32),
            pltpu.VMEM((rows, lanes), jnp.float32),
            pltpu.VMEM((TILE, lanes), jnp.float32),
            pltpu.SMEM((1,), jnp.float32),
            dma((3,)),
            dma((4 * tiles,)),
            dma((4 * tiles,)),
            dma((8,)),
            dma((8,)),
            dma((slabs * wedges,)),
            dma((slabs * wedges,)),
        ],
        compiler_params=pltpu.CompilerParams(collective_id=0, has_side_effects=True),
    )(core_mass, table, conserved)
    return advanced, mass.reshape(rows)


def solution(mesh):
    in_specs = (P(None, "radial", "phi", None), P())
    out_specs = (P(None, "radial", "phi", None), P("radial"))
    return jax.shard_map(body, mesh=mesh, in_specs=in_specs, out_specs=out_specs, check_vma=False)
```

profile of v0, /device:TPU:0, one launch (start us, length us, event | category | flops | bytes accessed | tf_op | source)
XLA Modules:
  0.0 23.4 jit_solution(6082257044391859857)
XLA Ops:
  1.3 20.8 %shard_map.50 = (f32[8,8,16,128]{3,2,1,0:T(8,128)S(1)}, f32[1,8]{1,0:T(1,128)S(1)}) custom-call(f32[1]{0:T(128)S(6)} %copy.9.core_ref, f32[8,128]{1,0:T(8,128)} %constant.2.clone.table_ref, f32[8,8,16,128]{3,2,1,0:T(8,128)} %input_ref.1), custom_call_target="tpu_custom_call" | custom-call | tf_op jit(solution)/shard_map/pallas_call | solution.py:478
  22.1 0.8 %copy.7 = f32[8,8,16,128]{3,2,1,0:T(8,128)} copy(f32[8,8,16,128]{3,2,1,0:T(8,128)S(1)} %get-tuple-element.6) | data formatting | bytes 1048576
  22.9 0.5 %copy.8 = f32[8]{0:T(128)} copy(f32[8]{0:T(128)S(1)} %bitcast.1) | data formatting | bytes 64
where the time goes:
time: 23.5 us; the launch traced here: 23.4 us
  Pallas kernels  20.8 us (89%)
  local copies, waits for them, and re-layouts  1.31 us (6%)
  between operations  1.28 us (5%)
    pallas_call x1, Pallas kernels, body(): pl.pallas_call(functools.partial(kernel, sizes, (slabs, wedges)), out_sha...  20.8 us
    unnamed x2, local copies, waits for them, and re-layouts  1.31 us

commit v1 on v0

v1 whole, which is shorter than its diff:
```python
import functools
import math

import jax
import jax.numpy as jnp
import numpy as np
from jax import lax
from jax.experimental import pallas as pl
from jax.experimental.pallas import tpu as pltpu
from jax.sharding import PartitionSpec as P

ADIABATIC = 4.0 / 3.0
INNER_RADIUS = 1.0
OUTER_RADIUS = 2.0
COURANT = 0.4
GRAVITY_KICK = 0.004
MINIMUM_DENSITY = 0.05
PRESSURE_FLOOR = 0.01
MESH = pl.DeviceIdType.MESH
TILE = 8
PAD = 8


def step_sizes(radial_total, phi_total, theta_total):
    theta_step = math.pi / theta_total
    phi_step = 2.0 * math.pi / phi_total
    polar_width = INNER_RADIUS * math.sin(0.5 * theta_step) * phi_step
    radial_step = min(2.0 * polar_width, (OUTER_RADIUS - INNER_RADIUS) / radial_total)
    timestep = COURANT * min(radial_step, polar_width)
    return (radial_step, theta_step, phi_step, timestep)


def angle_tables(theta_cells, theta_step):
    step = np.float32(theta_step)
    centre = (np.arange(theta_cells, dtype=np.float32) + np.float32(0.5)) * step
    face = np.arange(theta_cells + 1, dtype=np.float32) * step
    sine = np.sin(centre.astype(np.float64))
    cosine = np.cos(centre.astype(np.float64))
    face_sine = np.sin(face.astype(np.float64))
    zero = np.zeros(theta_cells)
    rows = [sine, face_sine[:-1], face_sine[1:], cosine / sine, 1.0 / sine, zero, zero, zero]
    return np.stack(rows).astype(np.float32)


def half_slope(below, above):
    return 0.5 * (
        jnp.maximum(jnp.minimum(below, above), 0.0) + jnp.minimum(jnp.maximum(below, above), 0.0)
    )


def thermo(q):
    density = jnp.maximum(q[0], MINIMUM_DENSITY)
    inverse = 1.0 / density
    kinetic = 0.5 * (q[1] * q[1] + q[2] * q[2] + q[3] * q[3]) * inverse
    pressure = jnp.maximum((ADIABATIC - 1.0) * (q[4] - kinetic), PRESSURE_FLOOR * density)
    return density, inverse, pressure


def physical(q, component):
    _, inverse, pressure = thermo(q)
    normal = q[component] * inverse
    squared = ADIABATIC * pressure * inverse
    return normal, pressure, jnp.abs(normal) + squared * lax.rsqrt(squared)


def flux(left, right, component):
    left_v, left_p, left_a = physical(left, component)
    right_v, right_p, right_a = physical(right, component)
    signal = jnp.maximum(left_a, right_a)
    left_w = 0.5 * (left_v + signal)
    right_w = 0.5 * (right_v - signal)
    out = [a * left_w + b * right_w for a, b in zip(left, right)]
    out[component] = out[component] + 0.5 * (left_p + right_p)
    out[4] = out[4] + 0.5 * (left_p * left_v + right_p * right_v)
    return out


def two_faces(rows, component):
    lower_left, lower_right, upper_left, upper_right = [], [], [], []
    for a, b, c, d, e in zip(*rows):
        ab, bc, cd, de = b - a, c - b, d - c, e - d
        sb, sc, sd = half_slope(ab, bc), half_slope(bc, cd), half_slope(cd, de)
        lower_left.append(b + sb)
        lower_right.append(c - sc)
        upper_left.append(c + sc)
        upper_right.append(d - sd)
    return flux(lower_left, lower_right, component), flux(upper_left, upper_right, component)


def kernel(
    sizes,
    counts,
    core_ref,
    table_ref,
    input_ref,
    out_ref,
    mass_ref,
    first,
    second,
    edge,
    halo,
    part,
    slab_part,
    wedge_got,
    slab_got,
    heavy,
    pull,
    table,
    core,
    load_sem,
    radial_send,
    radial_recv,
    phi_send,
    phi_recv,
    wedge_send,
    wedge_recv,
    slab_send,
    slab_recv,
    radial_ready,
    phi_ready,
):
    radial_step, theta_step, phi_step, timestep = sizes
    slabs, wedges = counts
    variables, rows, cells, lanes = input_ref.shape
    tiles = cells // TILE
    strength = GRAVITY_KICK / timestep
    slab, wedge = lax.axis_index("radial"), lax.axis_index("phi")
    has_up, has_down = slab < slabs - 1, slab > 0

    def load(begin, count, sem):
        return pltpu.make_async_copy(
            input_ref.at[:, pl.ds(begin, count)],
            first.at[:, pl.ds(2 + begin, count), pl.ds(PAD, cells), :],
            load_sem.at[sem],
        )

    load_low, load_high, load_inside = load(0, 2, 0), load(rows - 2, 2, 1), load(2, rows - 4, 2)
    load_table = pltpu.make_async_copy(table_ref, table, load_sem.at[3])
    load_core = pltpu.make_async_copy(core_ref, core, load_sem.at[4])
    for copy in (load_low, load_high, load_inside, load_table, load_core):
        copy.start()
    slab_got[...] = jnp.zeros(slab_got.shape, jnp.float32)

    def radial_peer(jump):
        return (lax.rem(slab + jump + slabs, slabs), wedge)

    def phi_peer(jump):
        return (slab, lax.rem(wedge + jump + wedges, wedges))

    barrier = pltpu.get_barrier_semaphore()

    def signal(sem, peer, condition):
        @pl.when(condition)
        def _():
            pl.semaphore_signal(sem, inc=1, device_id=peer, device_id_type=MESH)

    for j in range(1, slabs):
        signal(barrier, radial_peer(j), slab + j < slabs)
    for j in range(1, wedges):
        signal(barrier, phi_peer(j), wedge + j < wedges)
    pl.when(slab + wedge > 0)(lambda: pl.semaphore_wait(barrier, slab + wedge))
    for j in range(1, wedges):
        signal(phi_ready.at[j], phi_peer(-j), wedge >= j)
    for j in range(1, slabs):
        signal(radial_ready.at[j], radial_peer(-j), slab >= j)

    def remote(src, dst, send, recv, peer):
        return pltpu.make_async_remote_copy(
            src_ref=src, dst_ref=dst, send_sem=send, recv_sem=recv, device_id=peer,
            device_id_type=MESH,
        )

    def radial_copies(buffer, section, tile):
        where = pl.ds(PAD + TILE * tile, TILE)
        slot = (section * tiles + tile) * 2
        up = remote(
            buffer.at[:, pl.ds(rows, 2), where, :], buffer.at[:, pl.ds(0, 2), where, :],
            radial_send.at[slot], radial_recv.at[slot], radial_peer(1),
        )
        down = remote(
            buffer.at[:, pl.ds(2, 2), where, :], buffer.at[:, pl.ds(rows + 2, 2), where, :],
            radial_send.at[slot + 1], radial_recv.at[slot + 1], radial_peer(-1),
        )
        return up, down

    first_radial = [radial_copies(first, 0, t) for t in range(tiles)]
    second_radial = [radial_copies(second, 1, t) for t in range(tiles)]

    def up_start(copies):
        pl.when(has_up)(copies[0].start)

    def down_start(copies):
        pl.when(has_down)(copies[1].start)

    whole, inside, low_edge, high_edge = (0, rows), (2, rows - 4), (0, 2), (rows - 2, 2)

    def phi_copies(section, piece, slot):
        where = pl.ds(*piece)
        return [
            remote(
                edge.at[section * 2 + side, :, where], halo.at[section * 2 + side, :, where],
                phi_send.at[slot + side], phi_recv.at[slot + side], phi_peer(jump),
            )
            for side, jump in ((0, -1), (1, 1))
        ]

    def phi_pack(buffer, section, side, piece):
        begin, count = piece
        start = PAD if side == 0 else PAD + cells - 2
        edge[section * 2 + side, :, pl.ds(begin, count)] = buffer[
            :, pl.ds(2 + begin, count), pl.ds(start, 2), :
        ]

    def phi_unpack(buffer, section, side, piece):
        begin, count = piece
        start = PAD + cells if side == 0 else PAD - 2
        buffer[:, pl.ds(2 + begin, count), pl.ds(start, 2), :] = halo[
            section * 2 + side, :, pl.ds(begin, count)
        ]

    first_phi = phi_copies(0, whole, 0)
    inside_phi = phi_copies(1, inside, 2)
    low_phi, high_phi = phi_copies(1, low_edge, 4), phi_copies(1, high_edge, 6)

    wedge_copies = [
        remote(part, wedge_got.at[j], wedge_send.at[j], wedge_recv.at[j], phi_peer(j))
        for j in range(1, wedges)
    ]
    slab_copies = {
        j: remote(slab_part, slab_got.at[j], slab_send.at[j], slab_recv.at[j], radial_peer(j))
        for j in range(1, slabs)
    }
    slab_back = remote(
        slab_part, slab_got.at[0], slab_send.at[0], slab_recv.at[0], radial_peer(-1)
    )

    load_low.wait()
    down_start(first_radial[0])
    load_high.wait()
    load_inside.wait()
    phi_pack(first, 0, 0, whole)
    phi_pack(first, 0, 1, whole)
    for j in range(1, wedges):
        @pl.when(wedge + j < wedges)
        def _():
            pl.semaphore_wait(phi_ready.at[j], 1)
    for copy in first_phi:
        copy.start()

    @pl.when(has_up)
    def _():
        pl.semaphore_wait(radial_ready.at[1], 1)
        for copies in first_radial:
            copies[0].start()

    for copies in first_radial[1:]:
        down_start(copies)

    load_table.wait()
    load_core.wait()
    shape = (TILE, lanes)
    lane = lax.broadcasted_iota(jnp.int32, (rows, lanes), 1)
    line = lax.broadcasted_iota(jnp.int32, (rows, lanes), 0)
    column = jnp.sum(first[0, pl.ds(2, rows), pl.ds(PAD, cells), :], axis=1)
    column = jnp.sum(column * table[0:1, :], axis=1, keepdims=True)
    centres = INNER_RADIUS + (
        (slab * rows + line).astype(jnp.float32) + 0.5
    ) * radial_step
    column = column * centres * centres * (radial_step * theta_step * phi_step)
    part[...] = jnp.sum(jnp.where(lane == line, column, 0.0), axis=0, keepdims=True)
    wedge_got[0] = part[...]
    for copy in wedge_copies:
        copy.start()

    lane_tile = lax.broadcasted_iota(jnp.int32, shape, 1)
    is_first, is_last = lane_tile == 0, lane_tile == lanes - 1

    def rate(buffer, r, tile, radial=True, around_phi=True, along_theta=True):
        start = PAD + TILE * tile

        def at(row, offset):
            where = pl.ds(start + offset, TILE)
            fields = [buffer.at[k] for k in range(variables)]
            if buffer is second:
                fields[1], fields[4] = heavy.at[0], heavy.at[1]
            return [field[row + 2, where, :] for field in fields]

        def spread(value):
            return jnp.broadcast_to(value, shape)

        index = jnp.full(shape, slab * rows + r, jnp.int32).astype(jnp.float32)
        radius = INNER_RADIUS + (index + 0.5) * radial_step
        inner, outer = radius - 0.5 * radial_step, radius + 0.5 * radial_step
        inverse_r = 1.0 / radius
        centre = at(r, 0)
        total = [0.0] * variables
        if radial:
            lower, upper = two_faces([at(r + o, 0) if o else centre for o in range(-2, 3)], 1)
            scale = inverse_r * inverse_r * (1.0 / radial_step)
            area_in, area_out = inner * inner * scale, outer * outer * scale
            total = [area_in * a - area_out * b for a, b in zip(lower, upper)]
        around = inverse_r * spread(table[4:5, :])
        if around_phi:
            lower, upper = two_faces([at(r, o) if o else centre for o in range(-2, 3)], 3)
            scale = around * (1.0 / phi_step)
            total = [t + (a - b) * scale for t, a, b in zip(total, lower, upper)]
        if not along_theta:
            return centre, total
        left, right = [], []
        for q in centre:
            after = jnp.where(is_last, q, pltpu.roll(q, lanes - 1, 1))
            above = after - q
            below = jnp.where(is_first, 0.0, pltpu.roll(above, 1, 1))
            slope = half_slope(below, above)
            left.append(q + slope)
            right.append(jnp.where(is_last, q, pltpu.roll(q - slope, lanes - 1, 1)))
        upper = flux(left, right, 2)
        scale = around * (1.0 / theta_step)
        low_sine, high_sine = spread(table[1:2, :]), spread(table[2:3, :])
        low_area, high_area = low_sine * scale, high_sine * scale
        total = [
            t + (low_area * pltpu.roll(f, 1, 1) - high_area * f) for t, f in zip(total, upper)
        ]
        density, inverse, pressure = thermo(centre)
        vr, vt, vp = (centre[m] * inverse for m in (1, 2, 3))
        cot = spread(table[3:4, :])
        total[1] = total[1] + (2.0 * pressure + density * (vt * vt + vp * vp)) * inverse_r
        total[2] = total[2] + (
            (pressure + density * vp * vp) * cot - density * vr * vt
        ) * inverse_r
        total[3] = total[3] - density * vp * (vr + vt * cot) * inverse_r
        return centre, total

    def first_pass(r, tile, radial):
        centre, total = rate(first, r, tile, radial=radial, around_phi=False)
        where = pl.ds(PAD + TILE * tile, TILE)
        for k in range(variables):
            second[k, r + 2, where, :] = centre[k] + timestep * total[k]

    def add_one(r, tile, **parts):
        _, total = rate(first, r, tile, along_theta=False, **parts)
        where = pl.ds(PAD + TILE * tile, TILE)
        for k in range(variables):
            second[k, r + 2, where, :] = second[k, r + 2, where, :] + timestep * total[k]

    def gravity(p, tile):
        where = pl.ds(PAD + TILE * tile, TILE)
        kick = timestep * jnp.broadcast_to(pull[pl.ds(p, 1), :], shape)
        density = jnp.maximum(first[0, p, where, :], MINIMUM_DENSITY)
        heavy[0, p, where, :] = second[1, p, where, :] - density * kick
        heavy[1, p, where, :] = second[4, p, where, :] - first[1, p, where, :] * kick

    def section_two(r, tile, radial=True):
        centre, total = rate(second, r, tile, radial=radial)
        force = jnp.broadcast_to(pull[pl.ds(r + 2, 1), :], shape)
        density = jnp.maximum(centre[0], MINIMUM_DENSITY)
        total[1] = total[1] - density * force
        total[4] = total[4] - centre[1] * force
        where = pl.ds(PAD + TILE * tile, TILE)
        into = pl.ds(TILE * tile, TILE)
        for k in range(variables):
            begin = first[k, r + 2, where, :]
            out_ref[k, r, into, :] = 0.5 * begin + 0.5 * (centre[k] + timestep * total[k])

    def radial_two(r, tile):
        _, total = rate(second, r, tile, around_phi=False, along_theta=False)
        into = pl.ds(TILE * tile, TILE)
        for k in range(variables):
            out_ref[k, r, into, :] = out_ref[k, r, into, :] + (0.5 * timestep) * total[k]

    def each_row(low, high, step):
        lax.fori_loop(low, high, lambda r, _: (step(r), 0)[1], 0)

    def each_edge(step):
        lax.fori_loop(
            0, 4, lambda i, _: (step(i + (i // 2) * (rows - 4)), 0)[1], 0
        )

    def all_tiles(step):
        def run(r):
            for t in range(tiles):
                step(r, t)

        return run

    def low_land(copies, buffer, tile, after=None):
        where = pl.ds(PAD + TILE * tile, TILE)

        @pl.when(has_down)
        def _():
            copies[0].wait_recv()
            if after:
                after(0, tile)
                after(1, tile)

        @pl.when(jnp.logical_not(has_down))
        def _():
            value = buffer[:, 2, where, :]
            buffer[:, 0, where, :] = value
            buffer[:, 1, where, :] = value
            if buffer is second:
                value = heavy[:, 2, where, :]
                heavy[:, 0, where, :] = value
                heavy[:, 1, where, :] = value

    def high_land(copies, buffer, tile, after=None):
        where = pl.ds(PAD + TILE * tile, TILE)

        @pl.when(has_up)
        def _():
            copies[1].wait_recv()
            if after:
                after(rows + 2, tile)
                after(rows + 3, tile)

        @pl.when(jnp.logical_not(has_up))
        def _():
            value = buffer[:, rows + 1, where, :]
            buffer[:, rows + 2, where, :] = value
            buffer[:, rows + 3, where, :] = value
            if buffer is second:
                value = heavy[:, rows + 1, where, :]
                heavy[:, rows + 2, where, :] = value
                heavy[:, rows + 3, where, :] = value

    def mass_start(low, high):
        for j in range(low, min(high, slabs)):
            @pl.when(slab + j < slabs)
            def _():
                if j > 1:
                    pl.semaphore_wait(radial_ready.at[j], 1)
                slab_copies[j].start()

    each_row(2, rows - 2, all_tiles(lambda r, t: first_pass(r, t, True)))
    for copy in wedge_copies:
        copy.wait_recv()
    shells = jnp.zeros((1, lanes), jnp.float32)
    for w in range(wedges):
        shells = shells + wedge_got[lax.rem(wedge + wedges - w, wedges)]
    slab_part[...] = shells
    pl.when(has_down)(slab_back.start)
    mass_start(1, 3)
    each_edge(all_tiles(lambda r, t: first_pass(r, t, False)))
    for side, copy in enumerate(first_phi):
        copy.wait_recv()
        phi_unpack(first, 0, side, whole)
    each_row(0, rows, all_tiles(lambda r, t: add_one(r, t, radial=False)))
    for side, copy in enumerate(inside_phi):
        phi_pack(second, 1, side, inside)
        copy.start()
    mass_start(3, 5)

    for t in range(tiles):
        low_land(first_radial[t], first, t)
        each_row(0, 2, lambda r: add_one(r, t, around_phi=False))
        down_start(second_radial[t])
    for t in range(tiles):
        high_land(first_radial[t], first, t)
        each_row(rows - 2, rows, lambda r: add_one(r, t, around_phi=False))
        up_start(second_radial[t])
    for side in range(2):
        phi_pack(second, 1, side, low_edge)
        low_phi[side].start()
        phi_pack(second, 1, side, high_edge)
        high_phi[side].start()
    mass_start(5, slabs)

    pl.when(has_up)(slab_back.wait_recv)
    for j in range(1, slabs):
        pl.when(slab >= j)(slab_copies[j].wait_recv)
    before = jnp.zeros((1, lanes), jnp.float32)
    for j in range(slabs - 1, 0, -1):
        before = before + slab_got[j]
    span = (rows + 4, lanes)
    lane = lax.broadcasted_iota(jnp.int32, span, 1)
    line = lax.broadcasted_iota(jnp.int32, span, 0) - 2

    def below(row):
        return jnp.where(lane < row, 1.0, jnp.where(lane == row, 0.5, 0.0))

    def above(row):
        return jnp.where(lane > row, 1.0, jnp.where(lane == row, 0.5, 0.0))

    enclosed = below(line) * slab_part[...] + below(line - rows) * slab_got[0]
    enclosed = enclosed + (before - above(line + rows) * slab_got[1])
    enclosed = core[0] + jnp.sum(enclosed, axis=1, keepdims=True) + jnp.zeros(span, jnp.float32)
    mass_ref[...] = jnp.sum(jnp.where(lane == line, enclosed, 0.0), axis=0, keepdims=True)[:, :rows]
    centres = INNER_RADIUS + (
        (slab * rows + line).astype(jnp.float32) + 0.5
    ) * radial_step
    pull[...] = strength * enclosed / (centres * centres)

    each_row(2, rows + 2, all_tiles(gravity))

    def phi_land(copies, piece):
        begin, count = piece
        for side in range(2):
            copies[side].wait_recv()
            phi_unpack(second, 1, side, piece)
            each_row(2 + begin, 2 + begin + count, lambda p: gravity(p, -1 if side else tiles))

    phi_land(inside_phi, inside)
    each_row(2, rows - 2, all_tiles(section_two))
    phi_land(low_phi, low_edge)
    phi_land(high_phi, high_edge)
    each_edge(all_tiles(lambda r, t: section_two(r, t, False)))
    for t in range(tiles):
        high_land(second_radial[t], second, t, gravity)
        each_row(rows - 2, rows, lambda r: radial_two(r, t))
    for t in range(tiles):
        low_land(second_radial[t], second, t, gravity)
        each_row(0, 2, lambda r: radial_two(r, t))

    for copy in wedge_copies + first_phi + inside_phi + low_phi + high_phi:
        copy.wait_send()
    for j in range(1, slabs):
        pl.when(slab + j < slabs)(slab_copies[j].wait_send)
    pl.when(has_down)(slab_back.wait_send)
    for up, down in first_radial + second_radial:
        pl.when(has_up)(up.wait_send)
        pl.when(has_down)(down.wait_send)


def store(advanced_ref, mass_ref, advanced_out, mass_out, sem):
    copies = [
        pltpu.make_async_copy(advanced_ref, advanced_out, sem.at[0]),
        pltpu.make_async_copy(mass_ref, mass_out, sem.at[1]),
    ]
    for copy in copies:
        copy.start()
    for copy in copies:
        copy.wait()


def body(conserved, core_mass):
    variables, rows, cells, lanes = conserved.shape
    slabs, wedges = lax.axis_size("radial"), lax.axis_size("phi")
    sizes = step_sizes(rows * slabs, cells * wedges, lanes)
    table = jnp.asarray(angle_tables(lanes, sizes[1]))
    tiles = cells // TILE
    padded = (variables, rows + 4, cells + 2 * PAD, lanes)
    vmem = pl.BlockSpec(memory_space=pltpu.VMEM)
    hbm = pl.BlockSpec(memory_space=pltpu.HBM)
    dma = pltpu.SemaphoreType.DMA
    advanced, mass = pl.pallas_call(
        functools.partial(kernel, sizes, (slabs, wedges)),
        out_shape=(
            pltpu.VMEM(conserved.shape, jnp.float32),
            pltpu.VMEM((1, rows), jnp.float32),
        ),
        in_specs=[pl.BlockSpec(memory_space=pl.ANY)] * 3,
        out_specs=(vmem, vmem),
        scratch_shapes=[
            pltpu.VMEM(padded, jnp.float32),
            pltpu.VMEM(padded, jnp.float32),
            pltpu.VMEM((4, variables, rows, 2, lanes), jnp.float32),
            pltpu.VMEM((4, variables, rows, 2, lanes), jnp.float32),
            pltpu.VMEM((1, lanes), jnp.float32),
            pltpu.VMEM((1, lanes), jnp.float32),
            pltpu.VMEM((wedges, 1, lanes), jnp.float32),
            pltpu.VMEM((slabs, 1, lanes), jnp.float32),
            pltpu.VMEM((2,) + padded[1:], jnp.float32),
            pltpu.VMEM((rows + 4, lanes), jnp.float32),
            pltpu.VMEM((TILE, lanes), jnp.float32),
            pltpu.SMEM((1,), jnp.float32),
            dma((5,)),
            dma((4 * tiles,)),
            dma((4 * tiles,)),
            dma((8,)),
            dma((8,)),
            dma((wedges,)),
            dma((wedges,)),
            dma((slabs,)),
            dma((slabs,)),
            pltpu.SemaphoreType.REGULAR((slabs,)),
            pltpu.SemaphoreType.REGULAR((wedges,)),
        ],
        compiler_params=pltpu.CompilerParams(collective_id=0, has_side_effects=True),
    )(core_mass, table, conserved)
    return pl.pallas_call(
        store,
        out_shape=(
            jax.ShapeDtypeStruct(conserved.shape, jnp.float32),
            jax.ShapeDtypeStruct((rows,), jnp.float32),
        ),
        in_specs=[pl.BlockSpec(memory_space=pl.ANY)] * 2,
        out_specs=(hbm, hbm),
        scratch_shapes=[dma((2,))],
        compiler_params=pltpu.CompilerParams(vmem_limit_bytes=4 * 2**20),
    )(advanced, mass.reshape(rows))


def solution(mesh):
    in_specs = (P(None, "radial", "phi", None), P())
    out_specs = (P(None, "radial", "phi", None), P("radial"))
    return jax.shard_map(body, mesh=mesh, in_specs=in_specs, out_specs=out_specs, check_vma=False)
```

time: 23.5 us -> 21.3 us (0.906)
  the two profiles are of different devices: /device:TPU:0 before, /device:TPU:28 now
where the time goes in v1:
time: 21.3 us; the launch traced here: 21.2 us
  Pallas kernels  19.9 us (93%)
  between operations  1.28 us (6%)
    pallas_call x1, Pallas kernels, body(): pl.pallas_call(functools.partial(kernel, sizes, (slabs, wedges)), out_sha...  19.1 us
    pallas_call x1, Pallas kernels, body(): pl.pallas_call(store, out_shape=(jax.ShapeDtypeStruct(conserved.shape, jn...  0.81 us

profile of v1, /device:TPU:28, one launch (start us, length us, event | category | flops | bytes accessed | tf_op | source)
XLA Modules:
  0.0 21.2 jit_solution(13872851197056796061)
XLA Ops:
  1.3 19.1 %shard_map.50 = (f32[8,8,16,128]{3,2,1,0:T(8,128)S(1)}, f32[1,8]{1,0:T(1,128)S(1)}) custom-call(f32[1]{0:T(128)S(6)} %copy.5.core_ref, f32[8,128]{1,0:T(8,128)} %constant.2.clone.table_ref, f32[8,8,16,128]{3,2,1,0:T(8,128)} %input_ref.1), custom_call_target="tpu_custom_call" | custom-call | tf_op jit(solution)/shard_map/pallas_call | solution.py:545
  20.4 0.8 %shard_map.51 = (f32[8,8,16,128]{3,2,1,0:T(8,128)}, f32[8]{0:T(128)}) custom-call(f32[8,8,16,128]{3,2,1,0:T(8,128)S(1)} %get-tuple-element.4.advanced_ref, f32[8]{0:T(128)S(1)} %bitcast.1), custom_call_target="tpu_custom_call" | custom-call | tf_op jit(solution)/shard_map/pallas_call | solution.py:580

commit v2 on v1

--- a/solution.py
+++ b/solution.py
@@ -116,8 +116,8 @@
     wedge_recv,
     slab_send,
     slab_recv,
-    radial_ready,
     phi_ready,
+    slab_ready,
 ):
     radial_step, theta_step, phi_step, timestep = sizes
     slabs, wedges = counts
@@ -125,27 +125,22 @@
     tiles = cells // TILE
     strength = GRAVITY_KICK / timestep
     slab, wedge = lax.axis_index("radial"), lax.axis_index("phi")
+    half = lax.rem(slab, 2)
+    is_outer, is_inner = half == 1, half == 0
     has_up, has_down = slab < slabs - 1, slab > 0
 
-    def load(begin, count, sem):
-        return pltpu.make_async_copy(
-            input_ref.at[:, pl.ds(begin, count)],
-            first.at[:, pl.ds(2 + begin, count), pl.ds(PAD, cells), :],
-            load_sem.at[sem],
-        )
-
-    load_low, load_high, load_inside = load(0, 2, 0), load(rows - 2, 2, 1), load(2, rows - 4, 2)
-    load_table = pltpu.make_async_copy(table_ref, table, load_sem.at[3])
-    load_core = pltpu.make_async_copy(core_ref, core, load_sem.at[4])
-    for copy in (load_low, load_high, load_inside, load_table, load_core):
+    load = pltpu.make_async_copy(
+        input_ref, first.at[:, pl.ds(2, rows), pl.ds(PAD, cells), :], load_sem.at[0]
+    )
+    load_table = pltpu.make_async_copy(table_ref, table, load_sem.at[1])
+    load_core = pltpu.make_async_copy(core_ref, core, load_sem.at[2])
+    for copy in (load, load_table, load_core):
         copy.start()
     slab_got[...] = jnp.zeros(slab_got.shape, jnp.float32)
 
-    def radial_peer(jump):
-        return (lax.rem(slab + jump + slabs, slabs), wedge)
-
-    def phi_peer(jump):
-        return (slab, lax.rem(wedge + jump + wedges, wedges))
+    def at_peer(jump, turn=0):
+        around = lax.rem(wedge + turn + wedges, wedges) if turn else wedge
+        return (lax.rem(slab + jump + slabs, slabs), around)
 
     barrier = pltpu.get_barrier_semaphore()
 
@@ -154,16 +149,13 @@
         def _():
             pl.semaphore_signal(sem, inc=1, device_id=peer, device_id_type=MESH)
 
-    for j in range(1, slabs):
-        signal(barrier, radial_peer(j), slab + j < slabs)
+    signal(barrier, at_peer(1), has_up)
+    signal(barrier, at_peer(-1), has_down)
     for j in range(1, wedges):
-        signal(barrier, phi_peer(j), wedge + j < wedges)
-    pl.when(slab + wedge > 0)(lambda: pl.semaphore_wait(barrier, slab + wedge))
-    for j in range(1, wedges):
-        signal(phi_ready.at[j], phi_peer(-j), wedge >= j)
-    for j in range(1, slabs):
-        signal(radial_ready.at[j], radial_peer(-j), slab >= j)
-
+        signal(barrier, at_peer(0, j), wedge + j < wedges)
+    for j in range(2, slabs):
+        signal(barrier, at_peer(j), slab + j < slabs)
+    greeted = wedge + slab + jnp.where(has_up, 1, 0)
     def remote(src, dst, send, recv, peer):
         return pltpu.make_async_remote_copy(
             src_ref=src, dst_ref=dst, send_sem=send, recv_sem=recv, device_id=peer,
@@ -175,11 +167,11 @@
         slot = (section * tiles + tile) * 2
         up = remote(
             buffer.at[:, pl.ds(rows, 2), where, :], buffer.at[:, pl.ds(0, 2), where, :],
-            radial_send.at[slot], radial_recv.at[slot], radial_peer(1),
+            radial_send.at[slot], radial_recv.at[slot], at_peer(1),
         )
         down = remote(
             buffer.at[:, pl.ds(2, 2), where, :], buffer.at[:, pl.ds(rows + 2, 2), where, :],
-            radial_send.at[slot + 1], radial_recv.at[slot + 1], radial_peer(-1),
+            radial_send.at[slot + 1], radial_recv.at[slot + 1], at_peer(-1),
         )
         return up, down
 
@@ -199,7 +191,7 @@
         return [
             remote(
                 edge.at[section * 2 + side, :, where], halo.at[section * 2 + side, :, where],
-                phi_send.at[slot + side], phi_recv.at[slot + side], phi_peer(jump),
+                phi_send.at[slot + side], phi_recv.at[slot + side], at_peer(0, jump),
             )
             for side, jump in ((0, -1), (1, 1))
         ]
@@ -223,41 +215,20 @@
     low_phi, high_phi = phi_copies(1, low_edge, 4), phi_copies(1, high_edge, 6)
 
     wedge_copies = [
-        remote(part, wedge_got.at[j], wedge_send.at[j], wedge_recv.at[j], phi_peer(j))
+        remote(part, wedge_got.at[j], wedge_send.at[j], wedge_recv.at[j], at_peer(0, j))
         for j in range(1, wedges)
     ]
     slab_copies = {
-        j: remote(slab_part, slab_got.at[j], slab_send.at[j], slab_recv.at[j], radial_peer(j))
+        j: remote(slab_part, slab_got.at[j], slab_send.at[j], slab_recv.at[j], at_peer(j))
         for j in range(1, slabs)
     }
     slab_back = remote(
-        slab_part, slab_got.at[0], slab_send.at[0], slab_recv.at[0], radial_peer(-1)
+        slab_part, slab_got.at[0], slab_send.at[0], slab_recv.at[0], at_peer(-1)
     )
-
-    load_low.wait()
-    down_start(first_radial[0])
-    load_high.wait()
-    load_inside.wait()
-    phi_pack(first, 0, 0, whole)
-    phi_pack(first, 0, 1, whole)
-    for j in range(1, wedges):
-        @pl.when(wedge + j < wedges)
-        def _():
-            pl.semaphore_wait(phi_ready.at[j], 1)
-    for copy in first_phi:
-        copy.start()
-
-    @pl.when(has_up)
-    def _():
-        pl.semaphore_wait(radial_ready.at[1], 1)
-        for copies in first_radial:
-            copies[0].start()
-
-    for copies in first_radial[1:]:
-        down_start(copies)
-
+    beside = ((0, wedges - 1), (1, 1))
+
+    load.wait()
     load_table.wait()
-    load_core.wait()
     shape = (TILE, lanes)
     lane = lax.broadcasted_iota(jnp.int32, (rows, lanes), 1)
     line = lax.broadcasted_iota(jnp.int32, (rows, lanes), 0)
@@ -269,8 +240,8 @@
     column = column * centres * centres * (radial_step * theta_step * phi_step)
     part[...] = jnp.sum(jnp.where(lane == line, column, 0.0), axis=0, keepdims=True)
     wedge_got[0] = part[...]
-    for copy in wedge_copies:
-        copy.start()
+    phi_pack(first, 0, 0, whole)
+    phi_pack(first, 0, 1, whole)
 
     lane_tile = lax.broadcasted_iota(jnp.int32, shape, 1)
     is_first, is_last = lane_tile == 0, lane_tile == lanes - 1
@@ -423,48 +394,105 @@
                 heavy[:, rows + 2, where, :] = value
                 heavy[:, rows + 3, where, :] = value
 
-    def mass_start(low, high):
+    def slab_start(low, high):
         for j in range(low, min(high, slabs)):
             @pl.when(slab + j < slabs)
             def _():
                 if j > 1:
-                    pl.semaphore_wait(radial_ready.at[j], 1)
+                    pl.semaphore_wait(slab_ready.at[j], 1)
                 slab_copies[j].start()
 
-    each_row(2, rows - 2, all_tiles(lambda r, t: first_pass(r, t, True)))
+    def interior_one(r, t):
+        first_pass(r, t, True)
+
+    def edge_one(r, t):
+        first_pass(r, t, False)
+
+    split = jnp.where(has_down, 2, rows - 2)
+    each_row(0, 1, all_tiles(edge_one))
+    each_row(2, split, all_tiles(interior_one))
+    pl.when(greeted > 0)(lambda: pl.semaphore_wait(barrier, greeted))
+    for j in range(1, wedges):
+        signal(phi_ready.at[j], at_peer(0, -j), wedge >= j)
+    for j in range(2, slabs):
+        signal(slab_ready.at[j], at_peer(-j), slab >= j)
+
+    def first_down():
+        for copies in first_radial:
+            down_start(copies)
+
+    for j in range(1, wedges):
+        pl.when(wedge + j >= wedges)(wedge_copies[j - 1].start)
+    pl.when(is_inner)(first_down)
+    for copies in first_radial:
+        up_start(copies)
+    pl.when(is_outer)(first_down)
+    for side, jump in beside:
+        pl.when(wedge + jump >= wedges)(first_phi[side].start)
+    lax.fori_loop(
+        0, 3, lambda i, _: (all_tiles(edge_one)(jnp.where(i == 0, 1, rows - 3 + i)), 0)[1], 0
+    )
+    for j in range(1, wedges):
+        @pl.when(wedge + j < wedges)
+        def _():
+            pl.semaphore_wait(phi_ready.at[j], 1)
+            wedge_copies[j - 1].start()
+    for side, jump in beside:
+        pl.when(wedge + jump < wedges)(first_phi[side].start)
+    each_row(split, rows - 2, all_tiles(interior_one))
     for copy in wedge_copies:
         copy.wait_recv()
-    shells = jnp.zeros((1, lanes), jnp.float32)
+    own = jnp.zeros((1, lanes), jnp.float32)
     for w in range(wedges):
-        shells = shells + wedge_got[lax.rem(wedge + wedges - w, wedges)]
-    slab_part[...] = shells
+        own = own + wedge_got[lax.rem(wedge + wedges - w, wedges)]
+    slab_part[...] = own
     pl.when(has_down)(slab_back.start)
-    mass_start(1, 3)
-    each_edge(all_tiles(lambda r, t: first_pass(r, t, False)))
+    slab_start(1, 4)
     for side, copy in enumerate(first_phi):
         copy.wait_recv()
         phi_unpack(first, 0, side, whole)
-    each_row(0, rows, all_tiles(lambda r, t: add_one(r, t, radial=False)))
+    each_edge(all_tiles(lambda r, t: add_one(r, t, radial=False)))
+
+    def radial_side(step, copies, buffer, after, turn, send):
+        low = half == step
+        base = jnp.where(low, 0, rows - 2)
+        for t in range(tiles):
+            pl.when(low)(lambda: low_land(copies[t], buffer, t, after))
+            pl.when(jnp.logical_not(low))(lambda: high_land(copies[t], buffer, t, after))
+            each_row(0, 2, lambda i: turn(base + i, t))
+            if send:
+                pl.when(low)(lambda: down_start(send[t]))
+                pl.when(jnp.logical_not(low))(lambda: up_start(send[t]))
+
+    def radial_one(r, t):
+        add_one(r, t, around_phi=False)
+
+    radial_side(0, first_radial, first, None, radial_one, None)
+    slab_start(4, 6)
+    each_row(2, rows - 2, all_tiles(lambda r, t: add_one(r, t, radial=False)))
     for side, copy in enumerate(inside_phi):
         phi_pack(second, 1, side, inside)
         copy.start()
-    mass_start(3, 5)
-
     for t in range(tiles):
-        low_land(first_radial[t], first, t)
-        each_row(0, 2, lambda r: add_one(r, t, around_phi=False))
-        down_start(second_radial[t])
-    for t in range(tiles):
-        high_land(first_radial[t], first, t)
-        each_row(rows - 2, rows, lambda r: add_one(r, t, around_phi=False))
-        up_start(second_radial[t])
+        @pl.when(is_inner)
+        def _():
+            pl.when(has_up)(first_radial[t][0].wait_send)
+            down_start(second_radial[t])
+
+        @pl.when(is_outer)
+        def _():
+            pl.when(has_down)(first_radial[t][1].wait_send)
+            up_start(second_radial[t])
+
+    slab_start(6, slabs)
+    radial_side(1, first_radial, first, None, radial_one, second_radial)
     for side in range(2):
         phi_pack(second, 1, side, low_edge)
         low_phi[side].start()
         phi_pack(second, 1, side, high_edge)
         high_phi[side].start()
-    mass_start(5, slabs)
-
+
+    load_core.wait()
     pl.when(has_up)(slab_back.wait_recv)
     for j in range(1, slabs):
         pl.when(slab >= j)(slab_copies[j].wait_recv)
@@ -504,19 +532,18 @@
     phi_land(low_phi, low_edge)
     phi_land(high_phi, high_edge)
     each_edge(all_tiles(lambda r, t: section_two(r, t, False)))
-    for t in range(tiles):
-        high_land(second_radial[t], second, t, gravity)
-        each_row(rows - 2, rows, lambda r: radial_two(r, t))
-    for t in range(tiles):
-        low_land(second_radial[t], second, t, gravity)
-        each_row(0, 2, lambda r: radial_two(r, t))
+    radial_side(0, second_radial, second, gravity, radial_two, None)
+    radial_side(1, second_radial, second, gravity, radial_two, None)
 
     for copy in wedge_copies + first_phi + inside_phi + low_phi + high_phi:
         copy.wait_send()
     for j in range(1, slabs):
         pl.when(slab + j < slabs)(slab_copies[j].wait_send)
     pl.when(has_down)(slab_back.wait_send)
-    for up, down in first_radial + second_radial:
+    for up, down in first_radial:
+        pl.when(has_up & is_outer)(up.wait_send)
+        pl.when(has_down & is_inner)(down.wait_send)
+    for up, down in second_radial:
         pl.when(has_up)(up.wait_send)
         pl.when(has_down)(down.wait_send)
 
@@ -563,7 +590,7 @@
             pltpu.VMEM((rows + 4, lanes), jnp.float32),
             pltpu.VMEM((TILE, lanes), jnp.float32),
             pltpu.SMEM((1,), jnp.float32),
-            dma((5,)),
+            dma((3,)),
             dma((4 * tiles,)),
             dma((4 * tiles,)),
             dma((8,)),
@@ -572,8 +599,8 @@
             dma((wedges,)),
             dma((slabs,)),
             dma((slabs,)),
+            pltpu.SemaphoreType.REGULAR((wedges,)),
             pltpu.SemaphoreType.REGULAR((slabs,)),
-            pltpu.SemaphoreType.REGULAR((wedges,)),
         ],
         compiler_params=pltpu.CompilerParams(collective_id=0, has_side_effects=True),
     )(core_mass, table, conserved)

time: 21.3 us -> 20.1 us (0.944)
  the two profiles are of different devices: /device:TPU:28 before, /device:TPU:13 now
where the time goes in v2:
time: 20.1 us; the launch traced here: 19.8 us
  Pallas kernels  18.6 us (93%)
  between operations  1.28 us (6%)
    pallas_call x1, Pallas kernels, body(): pl.pallas_call(functools.partial(kernel, sizes, (slabs, wedges)), out_sha...  17.7 us
    pallas_call x1, Pallas kernels, body(): pl.pallas_call(store, out_shape=(jax.ShapeDtypeStruct(conserved.shape, jn...  0.81 us

profile of v2, /device:TPU:13, one launch (start us, length us, event | category | flops | bytes accessed | tf_op | source)
XLA Modules:
  0.0 19.8 jit_solution(2419580961067250945)
XLA Ops:
  1.3 17.7 %shard_map.50 = (f32[8,8,16,128]{3,2,1,0:T(8,128)S(1)}, f32[1,8]{1,0:T(1,128)S(1)}) custom-call(f32[1]{0:T(128)S(6)} %copy.5.core_ref, f32[8,128]{1,0:T(8,128)} %constant.2.clone.table_ref, f32[8,8,16,128]{3,2,1,0:T(8,128)} %input_ref.1), custom_call_target="tpu_custom_call" | custom-call | tf_op jit(solution)/shard_map/pallas_call | solution.py:572
  19.0 0.8 %shard_map.51 = (f32[8,8,16,128]{3,2,1,0:T(8,128)}, f32[8]{0:T(128)}) custom-call(f32[8,8,16,128]{3,2,1,0:T(8,128)S(1)} %get-tuple-element.4.advanced_ref, f32[8]{0:T(128)S(1)} %bitcast.1), custom_call_target="tpu_custom_call" | custom-call | tf_op jit(solution)/shard_map/pallas_call | solution.py:607

commit v3 on v2

--- a/solution.py
+++ b/solution.py
@@ -184,7 +184,9 @@
     def down_start(copies):
         pl.when(has_down)(copies[1].start)
 
-    whole, inside, low_edge, high_edge = (0, rows), (2, rows - 4), (0, 2), (rows - 2, 2)
+    whole = (0, rows)
+    main = (jnp.where(is_inner, 0, 2), rows - 2)
+    late = (jnp.where(is_inner, rows - 2, 0), 2)
 
     def phi_copies(section, piece, slot):
         where = pl.ds(*piece)
@@ -211,8 +213,7 @@
         ]
 
     first_phi = phi_copies(0, whole, 0)
-    inside_phi = phi_copies(1, inside, 2)
-    low_phi, high_phi = phi_copies(1, low_edge, 4), phi_copies(1, high_edge, 6)
+    main_phi, late_phi = phi_copies(1, main, 2), phi_copies(1, late, 4)
 
     wedge_copies = [
         remote(part, wedge_got.at[j], wedge_send.at[j], wedge_recv.at[j], at_peer(0, j))
@@ -321,8 +322,8 @@
         heavy[0, p, where, :] = second[1, p, where, :] - density * kick
         heavy[1, p, where, :] = second[4, p, where, :] - first[1, p, where, :] * kick
 
-    def section_two(r, tile, radial=True):
-        centre, total = rate(second, r, tile, radial=radial)
+    def theta_two(r, tile):
+        centre, total = rate(second, r, tile, radial=False, around_phi=False)
         force = jnp.broadcast_to(pull[pl.ds(r + 2, 1), :], shape)
         density = jnp.maximum(centre[0], MINIMUM_DENSITY)
         total[1] = total[1] - density * force
@@ -333,6 +334,12 @@
             begin = first[k, r + 2, where, :]
             out_ref[k, r, into, :] = 0.5 * begin + 0.5 * (centre[k] + timestep * total[k])
 
+    def phi_two(r, tile):
+        _, total = rate(second, r, tile, radial=False, along_theta=False)
+        into = pl.ds(TILE * tile, TILE)
+        for k in range(variables):
+            out_ref[k, r, into, :] = out_ref[k, r, into, :] + (0.5 * timestep) * total[k]
+
     def radial_two(r, tile):
         _, total = rate(second, r, tile, around_phi=False, along_theta=False)
         into = pl.ds(TILE * tile, TILE)
@@ -408,7 +415,7 @@
     def edge_one(r, t):
         first_pass(r, t, False)
 
-    split = jnp.where(has_down, 2, rows - 2)
+    split = jnp.where(slab + wedge > 0, 2, rows - 2)
     each_row(0, 1, all_tiles(edge_one))
     each_row(2, split, all_tiles(interior_one))
     pl.when(greeted > 0)(lambda: pl.semaphore_wait(barrier, greeted))
@@ -467,58 +474,25 @@
     def radial_one(r, t):
         add_one(r, t, around_phi=False)
 
-    radial_side(0, first_radial, first, None, radial_one, None)
-    slab_start(4, 6)
-    each_row(2, rows - 2, all_tiles(lambda r, t: add_one(r, t, radial=False)))
-    for side, copy in enumerate(inside_phi):
-        phi_pack(second, 1, side, inside)
-        copy.start()
-    for t in range(tiles):
-        @pl.when(is_inner)
-        def _():
-            pl.when(has_up)(first_radial[t][0].wait_send)
-            down_start(second_radial[t])
-
-        @pl.when(is_outer)
-        def _():
-            pl.when(has_down)(first_radial[t][1].wait_send)
-            up_start(second_radial[t])
-
-    slab_start(6, slabs)
-    radial_side(1, first_radial, first, None, radial_one, second_radial)
-    for side in range(2):
-        phi_pack(second, 1, side, low_edge)
-        low_phi[side].start()
-        phi_pack(second, 1, side, high_edge)
-        high_phi[side].start()
-
-    load_core.wait()
-    pl.when(has_up)(slab_back.wait_recv)
-    for j in range(1, slabs):
-        pl.when(slab >= j)(slab_copies[j].wait_recv)
-    before = jnp.zeros((1, lanes), jnp.float32)
-    for j in range(slabs - 1, 0, -1):
-        before = before + slab_got[j]
-    span = (rows + 4, lanes)
-    lane = lax.broadcasted_iota(jnp.int32, span, 1)
-    line = lax.broadcasted_iota(jnp.int32, span, 0) - 2
-
-    def below(row):
-        return jnp.where(lane < row, 1.0, jnp.where(lane == row, 0.5, 0.0))
-
-    def above(row):
-        return jnp.where(lane > row, 1.0, jnp.where(lane == row, 0.5, 0.0))
-
-    enclosed = below(line) * slab_part[...] + below(line - rows) * slab_got[0]
-    enclosed = enclosed + (before - above(line + rows) * slab_got[1])
-    enclosed = core[0] + jnp.sum(enclosed, axis=1, keepdims=True) + jnp.zeros(span, jnp.float32)
-    mass_ref[...] = jnp.sum(jnp.where(lane == line, enclosed, 0.0), axis=0, keepdims=True)[:, :rows]
-    centres = INNER_RADIUS + (
-        (slab * rows + line).astype(jnp.float32) + 0.5
-    ) * radial_step
-    pull[...] = strength * enclosed / (centres * centres)
-
-    each_row(2, rows + 2, all_tiles(gravity))
+    def row_of(i):
+        return jnp.where(is_inner, i, rows - 1 - i)
+
+    def each_from(low, high, step):
+        each_row(low, high, lambda i: step(row_of(i)))
+
+    def passing_start(copies, gates, which):
+        for t in range(tiles):
+            @pl.when(which)
+            def _():
+                pl.when(is_inner & has_up)(gates[t][0].wait_send)
+                pl.when(is_outer & has_down)(gates[t][1].wait_send)
+                pl.when(is_inner)(lambda: down_start(copies[t]))
+                pl.when(is_outer)(lambda: up_start(copies[t]))
+
+    def phi_leave(copies, piece):
+        for side, copy in enumerate(copies):
+            phi_pack(second, 1, side, piece)
+            copy.start()
 
     def phi_land(copies, piece):
         begin, count = piece
@@ -527,15 +501,68 @@
             phi_unpack(second, 1, side, piece)
             each_row(2 + begin, 2 + begin + count, lambda p: gravity(p, -1 if side else tiles))
 
-    phi_land(inside_phi, inside)
-    each_row(2, rows - 2, all_tiles(section_two))
-    phi_land(low_phi, low_edge)
-    phi_land(high_phi, high_edge)
-    each_edge(all_tiles(lambda r, t: section_two(r, t, False)))
+    span = (rows + 4, lanes)
+    lane = lax.broadcasted_iota(jnp.int32, span, 1)
+    line = lax.broadcasted_iota(jnp.int32, span, 0) - 2
+
+    def below(row):
+        return jnp.where(lane < row, 1.0, jnp.where(lane == row, 0.5, 0.0))
+
+    def above(row):
+        return jnp.where(lane > row, 1.0, jnp.where(lane == row, 0.5, 0.0))
+
+    further = INNER_RADIUS + (
+        (slab * rows + line).astype(jnp.float32) + 0.5
+    ) * radial_step
+
+    def masses():
+        load_core.wait()
+        for j in range(1, slabs):
+            pl.when(slab >= j)(slab_copies[j].wait_recv)
+        before = jnp.zeros((1, lanes), jnp.float32)
+        for j in range(slabs - 1, 0, -1):
+            before = before + slab_got[j]
+        enclosed = below(line) * slab_part[...] + (before - above(line + rows) * slab_got[1])
+        enclosed = core[0] + jnp.sum(enclosed, axis=1, keepdims=True) + jnp.zeros(span, jnp.float32)
+        mass_ref[...] = jnp.sum(jnp.where(lane == line, enclosed, 0.0), axis=0, keepdims=True)[:, :rows]
+        pull[...] = strength * enclosed / (further * further)
+
+        each_from(0, rows - 2, all_tiles(lambda r, t: gravity(r + 2, t)))
+
+    slab_start(4, 6)
+    radial_side(0, first_radial, first, None, radial_one, None)
+    slab_start(6, slabs)
+    each_row(2, rows - 2, all_tiles(lambda r, t: add_one(r, t, radial=False)))
+    phi_leave(main_phi, main)
+    passing_start(second_radial, first_radial, is_inner)
+    ahead = jnp.where(is_inner, rows - 4, 0)
+    pl.when(is_inner)(masses)
+    each_from(0, ahead, all_tiles(theta_two))
+    radial_side(1, first_radial, first, None, radial_one, None)
+    passing_start(second_radial, first_radial, is_outer)
+    for t in range(tiles):
+        pl.when(is_inner)(lambda: up_start(second_radial[t]))
+        pl.when(is_outer)(lambda: down_start(second_radial[t]))
+    phi_leave(late_phi, late)
+    pl.when(is_outer)(masses)
+    each_from(rows - 2, rows, all_tiles(lambda r, t: gravity(r + 2, t)))
+    each_from(ahead, rows, all_tiles(theta_two))
+    each_row(2, rows - 2, all_tiles(radial_two))
+    phi_land(main_phi, main)
+    each_from(0, rows - 2, all_tiles(phi_two))
+    phi_land(late_phi, late)
+    each_from(rows - 2, rows, all_tiles(phi_two))
+
+    @pl.when(has_up)
+    def _():
+        slab_back.wait_recv()
+        beyond = jnp.sum(below(line - rows) * slab_got[0], axis=1, keepdims=True)
+        pull[...] = pull[...] + strength * beyond / (further * further)
+
     radial_side(0, second_radial, second, gravity, radial_two, None)
     radial_side(1, second_radial, second, gravity, radial_two, None)
 
-    for copy in wedge_copies + first_phi + inside_phi + low_phi + high_phi:
+    for copy in wedge_copies + first_phi + main_phi + late_phi:
         copy.wait_send()
     for j in range(1, slabs):
         pl.when(slab + j < slabs)(slab_copies[j].wait_send)

time: 20.1 us -> 19 us (0.945)
  Pallas kernels: 18.6 us -> 17.5 us
    pallas_call x1, Pallas kernels: 17.7 us -> 16.7 us  [body(): pl.pallas_call(functools.partial(kernel, sizes, (slabs, wedges)), out_sha...]
where the time goes in v3:
time: 19 us; the launch traced here: 18.8 us
  Pallas kernels  17.5 us (92%)
  between operations  1.28 us (7%)
    pallas_call x1, Pallas kernels, body(): pl.pallas_call(functools.partial(kernel, sizes, (slabs, wedges)), out_sha...  16.7 us
    pallas_call x1, Pallas kernels, body(): pl.pallas_call(store, out_shape=(jax.ShapeDtypeStruct(conserved.shape, jn...  0.81 us

profile of v3, /device:TPU:13, one launch (start us, length us, event | category | flops | bytes accessed | tf_op | source)
XLA Modules:
  0.0 18.8 jit_solution(1813800902773992381)
XLA Ops:
  1.3 16.7 %shard_map.50 = (f32[8,8,16,128]{3,2,1,0:T(8,128)S(1)}, f32[1,8]{1,0:T(1,128)S(1)}) custom-call(f32[1]{0:T(128)S(6)} %copy.5.core_ref, f32[8,128]{1,0:T(8,128)} %constant.2.clone.table_ref, f32[8,8,16,128]{3,2,1,0:T(8,128)} %input_ref.1), custom_call_target="tpu_custom_call" | custom-call | tf_op jit(solution)/shard_map/pallas_call | solution.py:599
  18.0 0.8 %shard_map.51 = (f32[8,8,16,128]{3,2,1,0:T(8,128)}, f32[8]{0:T(128)}) custom-call(f32[8,8,16,128]{3,2,1,0:T(8,128)S(1)} %get-tuple-element.4.advanced_ref, f32[8]{0:T(128)S(1)} %bitcast.1), custom_call_target="tpu_custom_call" | custom-call | tf_op jit(solution)/shard_map/pallas_call | solution.py:634

commit v4 on v3

--- a/solution.py
+++ b/solution.py
@@ -112,10 +112,8 @@
     radial_recv,
     phi_send,
     phi_recv,
-    wedge_send,
-    wedge_recv,
-    slab_send,
-    slab_recv,
+    mass_send,
+    mass_recv,
     phi_ready,
     slab_ready,
 ):
@@ -162,16 +160,20 @@
             device_id_type=MESH,
         )
 
+    def await_bytes(ref, sem):
+        pltpu.make_async_copy(ref, ref, sem).wait()
+
     def radial_copies(buffer, section, tile):
         where = pl.ds(PAD + TILE * tile, TILE)
         slot = (section * tiles + tile) * 2
         up = remote(
             buffer.at[:, pl.ds(rows, 2), where, :], buffer.at[:, pl.ds(0, 2), where, :],
-            radial_send.at[slot], radial_recv.at[slot], at_peer(1),
+            radial_send.at[slot if section == 0 else 2 * tiles], radial_recv.at[slot], at_peer(1),
         )
         down = remote(
             buffer.at[:, pl.ds(2, 2), where, :], buffer.at[:, pl.ds(rows + 2, 2), where, :],
-            radial_send.at[slot + 1], radial_recv.at[slot + 1], at_peer(-1),
+            radial_send.at[slot + 1 if section == 0 else 2 * tiles], radial_recv.at[slot + 1],
+            at_peer(-1),
         )
         return up, down
 
@@ -193,7 +195,7 @@
         return [
             remote(
                 edge.at[section * 2 + side, :, where], halo.at[section * 2 + side, :, where],
-                phi_send.at[slot + side], phi_recv.at[slot + side], at_peer(0, jump),
+                phi_send.at[0], phi_recv.at[slot], at_peer(0, jump),
             )
             for side, jump in ((0, -1), (1, 1))
         ]
@@ -213,18 +215,18 @@
         ]
 
     first_phi = phi_copies(0, whole, 0)
-    main_phi, late_phi = phi_copies(1, main, 2), phi_copies(1, late, 4)
+    main_phi, late_phi = phi_copies(1, main, 1), phi_copies(1, late, 2)
 
     wedge_copies = [
-        remote(part, wedge_got.at[j], wedge_send.at[j], wedge_recv.at[j], at_peer(0, j))
+        remote(part, wedge_got.at[j], mass_send.at[0], mass_recv.at[0], at_peer(0, j))
         for j in range(1, wedges)
     ]
     slab_copies = {
-        j: remote(slab_part, slab_got.at[j], slab_send.at[j], slab_recv.at[j], at_peer(j))
+        j: remote(slab_part, slab_got.at[j], mass_send.at[1], mass_recv.at[1], at_peer(j))
         for j in range(1, slabs)
     }
     slab_back = remote(
-        slab_part, slab_got.at[0], slab_send.at[0], slab_recv.at[0], at_peer(-1)
+        slab_part, slab_got.at[0], mass_send.at[1], mass_recv.at[2], at_peer(-1)
     )
     beside = ((0, wedges - 1), (1, 1))
 
@@ -405,8 +407,9 @@
         for j in range(low, min(high, slabs)):
             @pl.when(slab + j < slabs)
             def _():
-                if j > 1:
-                    pl.semaphore_wait(slab_ready.at[j], 1)
+                if j > 1 and j % 2 == 0:
+                    others = 1 if j + 1 >= slabs else 1 + (slab + j + 1 < slabs).astype(jnp.int32)
+                    pl.semaphore_wait(slab_ready.at[j // 2 - 1], others)
                 slab_copies[j].start()
 
     def interior_one(r, t):
@@ -420,9 +423,9 @@
     each_row(2, split, all_tiles(interior_one))
     pl.when(greeted > 0)(lambda: pl.semaphore_wait(barrier, greeted))
     for j in range(1, wedges):
-        signal(phi_ready.at[j], at_peer(0, -j), wedge >= j)
+        signal(phi_ready.at[0], at_peer(0, -j), wedge >= j)
     for j in range(2, slabs):
-        signal(slab_ready.at[j], at_peer(-j), slab >= j)
+        signal(slab_ready.at[j // 2 - 1], at_peer(-j), slab >= j)
 
     def first_down():
         for copies in first_radial:
@@ -439,24 +442,25 @@
     lax.fori_loop(
         0, 3, lambda i, _: (all_tiles(edge_one)(jnp.where(i == 0, 1, rows - 3 + i)), 0)[1], 0
     )
+
+    @pl.when(wedge + 1 < wedges)
+    def _():
+        pl.semaphore_wait(phi_ready.at[0], wedges - 1 - wedge)
+
     for j in range(1, wedges):
-        @pl.when(wedge + j < wedges)
-        def _():
-            pl.semaphore_wait(phi_ready.at[j], 1)
-            wedge_copies[j - 1].start()
+        pl.when(wedge + j < wedges)(wedge_copies[j - 1].start)
     for side, jump in beside:
         pl.when(wedge + jump < wedges)(first_phi[side].start)
     each_row(split, rows - 2, all_tiles(interior_one))
-    for copy in wedge_copies:
-        copy.wait_recv()
+    await_bytes(wedge_got.at[pl.ds(1, wedges - 1)], mass_recv.at[0])
     own = jnp.zeros((1, lanes), jnp.float32)
     for w in range(wedges):
         own = own + wedge_got[lax.rem(wedge + wedges - w, wedges)]
     slab_part[...] = own
     pl.when(has_down)(slab_back.start)
     slab_start(1, 4)
-    for side, copy in enumerate(first_phi):
-        copy.wait_recv()
+    await_bytes(halo.at[pl.ds(0, 2)], phi_recv.at[0])
+    for side in range(2):
         phi_unpack(first, 0, side, whole)
     each_edge(all_tiles(lambda r, t: add_one(r, t, radial=False)))
 
@@ -480,8 +484,8 @@
     def each_from(low, high, step):
         each_row(low, high, lambda i: step(row_of(i)))
 
-    def passing_start(copies, gates, which):
-        for t in range(tiles):
+    def passing_start(copies, gates, which, chosen):
+        for t in chosen:
             @pl.when(which)
             def _():
                 pl.when(is_inner & has_up)(gates[t][0].wait_send)
@@ -494,10 +498,10 @@
             phi_pack(second, 1, side, piece)
             copy.start()
 
-    def phi_land(copies, piece):
+    def phi_land(slot, piece):
         begin, count = piece
+        await_bytes(halo.at[pl.ds(2, 2), :, pl.ds(begin, count)], phi_recv.at[slot])
         for side in range(2):
-            copies[side].wait_recv()
             phi_unpack(second, 1, side, piece)
             each_row(2 + begin, 2 + begin + count, lambda p: gravity(p, -1 if side else tiles))
 
@@ -518,7 +522,10 @@
     def masses():
         load_core.wait()
         for j in range(1, slabs):
-            pl.when(slab >= j)(slab_copies[j].wait_recv)
+            @pl.when(slab == j)
+            def _():
+                await_bytes(slab_got.at[pl.ds(1, j)], mass_recv.at[1])
+
         before = jnp.zeros((1, lanes), jnp.float32)
         for j in range(slabs - 1, 0, -1):
             before = before + slab_got[j]
@@ -532,14 +539,15 @@
     slab_start(4, 6)
     radial_side(0, first_radial, first, None, radial_one, None)
     slab_start(6, slabs)
+    passing_start(second_radial, first_radial, is_inner, range(tiles))
     each_row(2, rows - 2, all_tiles(lambda r, t: add_one(r, t, radial=False)))
     phi_leave(main_phi, main)
-    passing_start(second_radial, first_radial, is_inner)
+    passing_start(second_radial, first_radial, is_outer, range(1))
     ahead = jnp.where(is_inner, rows - 4, 0)
     pl.when(is_inner)(masses)
     each_from(0, ahead, all_tiles(theta_two))
     radial_side(1, first_radial, first, None, radial_one, None)
-    passing_start(second_radial, first_radial, is_outer)
+    passing_start(second_radial, first_radial, is_outer, range(1, tiles))
     for t in range(tiles):
         pl.when(is_inner)(lambda: up_start(second_radial[t]))
         pl.when(is_outer)(lambda: down_start(second_radial[t]))
@@ -548,9 +556,9 @@
     each_from(rows - 2, rows, all_tiles(lambda r, t: gravity(r + 2, t)))
     each_from(ahead, rows, all_tiles(theta_two))
     each_row(2, rows - 2, all_tiles(radial_two))
-    phi_land(main_phi, main)
+    phi_land(1, main)
     each_from(0, rows - 2, all_tiles(phi_two))
-    phi_land(late_phi, late)
+    phi_land(2, late)
     each_from(rows - 2, rows, all_tiles(phi_two))
 
     @pl.when(has_up)
@@ -562,17 +570,22 @@
     radial_side(0, second_radial, second, gravity, radial_two, None)
     radial_side(1, second_radial, second, gravity, radial_two, None)
 
-    for copy in wedge_copies + first_phi + main_phi + late_phi:
-        copy.wait_send()
-    for j in range(1, slabs):
-        pl.when(slab + j < slabs)(slab_copies[j].wait_send)
-    pl.when(has_down)(slab_back.wait_send)
+    await_bytes(halo, phi_send.at[0])
+    await_bytes(wedge_got.at[pl.ds(1, wedges - 1)], mass_send.at[0])
+    for j in range(slabs):
+        @pl.when(slab == j)
+        def _():
+            await_bytes(slab_got.at[pl.ds(0, slabs - 1 - j + min(j, 1))], mass_send.at[1])
+
     for up, down in first_radial:
         pl.when(has_up & is_outer)(up.wait_send)
         pl.when(has_down & is_inner)(down.wait_send)
-    for up, down in second_radial:
-        pl.when(has_up)(up.wait_send)
-        pl.when(has_down)(down.wait_send)
+    def second_sent(sides):
+        moved = second.at[:, pl.ds(0, 2 * sides), pl.ds(PAD, cells), :]
+        await_bytes(moved, radial_send.at[2 * tiles])
+
+    pl.when(has_up & has_down)(lambda: second_sent(2))
+    pl.when(has_up != has_down)(lambda: second_sent(1))
 
 
 def store(advanced_ref, mass_ref, advanced_out, mass_out, sem):
@@ -618,16 +631,14 @@
             pltpu.VMEM((TILE, lanes), jnp.float32),
             pltpu.SMEM((1,), jnp.float32),
             dma((3,)),
+            dma((2 * tiles + 1,)),
             dma((4 * tiles,)),
-            dma((4 * tiles,)),
-            dma((8,)),
-            dma((8,)),
-            dma((wedges,)),
-            dma((wedges,)),
-            dma((slabs,)),
-            dma((slabs,)),
-            pltpu.SemaphoreType.REGULAR((wedges,)),
-            pltpu.SemaphoreType.REGULAR((slabs,)),
+            dma((1,)),
+            dma((3,)),
+            dma((2,)),
+            dma((3,)),
+            pltpu.SemaphoreType.REGULAR((1,)),
+            pltpu.SemaphoreType.REGULAR((max(slabs // 2, 1),)),
         ],
         compiler_params=pltpu.CompilerParams(collective_id=0, has_side_effects=True),
     )(core_mass, table, conserved)

time: 19 us -> 18.3 us (0.963)
  Pallas kernels: 17.5 us -> 16.9 us
    pallas_call x1, Pallas kernels: 16.7 us -> 16 us  [body(): pl.pallas_call(functools.partial(kernel, sizes, (slabs, wedges)), out_sha...]
where the time goes in v4:
time: 18.3 us; the launch traced here: 18.1 us
  Pallas kernels  16.9 us (92%)
  between operations  1.28 us (7%)
    pallas_call x1, Pallas kernels, body(): pl.pallas_call(functools.partial(kernel, sizes, (slabs, wedges)), out_sha...  16 us
    pallas_call x1, Pallas kernels, body(): pl.pallas_call(store, out_shape=(jax.ShapeDtypeStruct(conserved.shape, jn...  0.81 us

profile of v4, /device:TPU:13, one launch (start us, length us, event | category | flops | bytes accessed | tf_op | source)
XLA Modules:
  0.0 18.1 jit_solution(8152502652716231078)
XLA Ops:
  1.3 16.0 %shard_map.50 = (f32[8,8,16,128]{3,2,1,0:T(8,128)S(1)}, f32[1,8]{1,0:T(1,128)S(1)}) custom-call(f32[1]{0:T(128)S(6)} %copy.5.core_ref, f32[8,128]{1,0:T(8,128)} %constant.2.clone.table_ref, f32[8,8,16,128]{3,2,1,0:T(8,128)} %input_ref.1), custom_call_target="tpu_custom_call" | custom-call | tf_op jit(solution)/shard_map/pallas_call | solution.py:612
  17.3 0.8 %shard_map.51 = (f32[8,8,16,128]{3,2,1,0:T(8,128)}, f32[8]{0:T(128)}) custom-call(f32[8,8,16,128]{3,2,1,0:T(8,128)S(1)} %get-tuple-element.4.advanced_ref, f32[8]{0:T(128)S(1)} %bitcast.1), custom_call_target="tpu_custom_call" | custom-call | tf_op jit(solution)/shard_map/pallas_call | solution.py:645

commit v5 on v4

--- a/solution.py
+++ b/solution.py
@@ -43,8 +43,8 @@
 
 
 def half_slope(below, above):
-    return 0.5 * (
-        jnp.maximum(jnp.minimum(below, above), 0.0) + jnp.minimum(jnp.maximum(below, above), 0.0)
+    return 0.5 * jnp.maximum(
+        jnp.minimum(below, above), jnp.minimum(jnp.maximum(below, above), 0.0)
     )
 
 
@@ -85,6 +85,15 @@
         upper_left.append(c + sc)
         upper_right.append(d - sd)
     return flux(lower_left, lower_right, component), flux(upper_left, upper_right, component)
+
+
+def one_face(rows, component):
+    left, right = [], []
+    for a, b, c, d in zip(*rows):
+        ab, bc, cd = b - a, c - b, d - c
+        left.append(b + half_slope(ab, bc))
+        right.append(c - half_slope(bc, cd))
+    return flux(left, right, component)
 
 
 def kernel(
@@ -249,30 +258,63 @@
     lane_tile = lax.broadcasted_iota(jnp.int32, shape, 1)
     is_first, is_last = lane_tile == 0, lane_tile == lanes - 1
 
-    def rate(buffer, r, tile, radial=True, around_phi=True, along_theta=True):
+    def fields_at(buffer, row, start):
+        where = pl.ds(start, TILE)
+        fields = [buffer.at[k] for k in range(variables)]
+        if buffer is second:
+            fields[1], fields[4] = heavy.at[0], heavy.at[1]
+        return [field[row + 2, where, :] for field in fields]
+
+    def radius_at(position):
+        step = jnp.full(shape, slab * rows + position, jnp.int32).astype(jnp.float32)
+        return INNER_RADIUS + step * radial_step
+
+    def face_scale(face, row):
+        area, inverse_r = radius_at(face), 1.0 / (radius_at(row) + 0.5 * radial_step)
+        return area * area * (inverse_r * inverse_r * (1.0 / radial_step))
+
+    def add_flux(buffer, row, tile, scale, values):
+        if buffer is first:
+            target, row, start, step = second, row + 2, PAD + TILE * tile, timestep
+        else:
+            target, start, step = out_ref, TILE * tile, 0.5 * timestep
+        scale = scale * step
+        where = pl.ds(start, TILE)
+        for k in range(variables):
+            target[k, row, where, :] = target[k, row, where, :] + scale * values[k]
+
+    def inner_face(buffer, face, tile):
         start = PAD + TILE * tile
+        values = one_face([fields_at(buffer, face + o, start) for o in range(-2, 2)], 1)
+        add_flux(buffer, face - 1, tile, -face_scale(face, face - 1), values)
+        add_flux(buffer, face, tile, face_scale(face, face), values)
+
+    def side_faces(buffer, low, tile):
+        start = PAD + TILE * tile
+        edge_row = jnp.where(low, 0, rows - 1)
+        next_row = jnp.where(low, 1, rows - 2)
+        lower, upper = two_faces([fields_at(buffer, edge_row + o, start) for o in range(-2, 3)], 1)
+        low_scale, high_scale = face_scale(edge_row, edge_row), face_scale(edge_row + 1, edge_row)
+        values = [low_scale * a - high_scale * b for a, b in zip(lower, upper)]
+        add_flux(buffer, edge_row, tile, 1.0, values)
+        between = [jnp.where(low, b, a) for a, b in zip(lower, upper)]
+        scale = face_scale(jnp.where(low, 1, rows - 1), next_row)
+        add_flux(buffer, next_row, tile, jnp.where(low, scale, -scale), between)
+
+    def rate(buffer, r, tile, around_phi=True, along_theta=True):
+        start = PAD + TILE * tile
 
         def at(row, offset):
-            where = pl.ds(start + offset, TILE)
-            fields = [buffer.at[k] for k in range(variables)]
-            if buffer is second:
-                fields[1], fields[4] = heavy.at[0], heavy.at[1]
-            return [field[row + 2, where, :] for field in fields]
+            return fields_at(buffer, row, start + offset)
 
         def spread(value):
             return jnp.broadcast_to(value, shape)
 
         index = jnp.full(shape, slab * rows + r, jnp.int32).astype(jnp.float32)
         radius = INNER_RADIUS + (index + 0.5) * radial_step
-        inner, outer = radius - 0.5 * radial_step, radius + 0.5 * radial_step
         inverse_r = 1.0 / radius
         centre = at(r, 0)
         total = [0.0] * variables
-        if radial:
-            lower, upper = two_faces([at(r + o, 0) if o else centre for o in range(-2, 3)], 1)
-            scale = inverse_r * inverse_r * (1.0 / radial_step)
-            area_in, area_out = inner * inner * scale, outer * outer * scale
-            total = [area_in * a - area_out * b for a, b in zip(lower, upper)]
         around = inverse_r * spread(table[4:5, :])
         if around_phi:
             lower, upper = two_faces([at(r, o) if o else centre for o in range(-2, 3)], 3)
@@ -305,14 +347,14 @@
         total[3] = total[3] - density * vp * (vr + vt * cot) * inverse_r
         return centre, total
 
-    def first_pass(r, tile, radial):
-        centre, total = rate(first, r, tile, radial=radial, around_phi=False)
+    def first_pass(r, tile):
+        centre, total = rate(first, r, tile, around_phi=False)
         where = pl.ds(PAD + TILE * tile, TILE)
         for k in range(variables):
             second[k, r + 2, where, :] = centre[k] + timestep * total[k]
 
-    def add_one(r, tile, **parts):
-        _, total = rate(first, r, tile, along_theta=False, **parts)
+    def phi_one(r, tile):
+        _, total = rate(first, r, tile, along_theta=False)
         where = pl.ds(PAD + TILE * tile, TILE)
         for k in range(variables):
             second[k, r + 2, where, :] = second[k, r + 2, where, :] + timestep * total[k]
@@ -325,7 +367,7 @@
         heavy[1, p, where, :] = second[4, p, where, :] - first[1, p, where, :] * kick
 
     def theta_two(r, tile):
-        centre, total = rate(second, r, tile, radial=False, around_phi=False)
+        centre, total = rate(second, r, tile, around_phi=False)
         force = jnp.broadcast_to(pull[pl.ds(r + 2, 1), :], shape)
         density = jnp.maximum(centre[0], MINIMUM_DENSITY)
         total[1] = total[1] - density * force
@@ -337,13 +379,7 @@
             out_ref[k, r, into, :] = 0.5 * begin + 0.5 * (centre[k] + timestep * total[k])
 
     def phi_two(r, tile):
-        _, total = rate(second, r, tile, radial=False, along_theta=False)
-        into = pl.ds(TILE * tile, TILE)
-        for k in range(variables):
-            out_ref[k, r, into, :] = out_ref[k, r, into, :] + (0.5 * timestep) * total[k]
-
-    def radial_two(r, tile):
-        _, total = rate(second, r, tile, around_phi=False, along_theta=False)
+        _, total = rate(second, r, tile, along_theta=False)
         into = pl.ds(TILE * tile, TILE)
         for k in range(variables):
             out_ref[k, r, into, :] = out_ref[k, r, into, :] + (0.5 * timestep) * total[k]
@@ -413,13 +449,12 @@
                 slab_copies[j].start()
 
     def interior_one(r, t):
-        first_pass(r, t, True)
-
-    def edge_one(r, t):
-        first_pass(r, t, False)
+        first_pass(r, t)
+        inner_face(first, r, t)
 
     split = jnp.where(slab + wedge > 0, 2, rows - 2)
-    each_row(0, 1, all_tiles(edge_one))
+    begun = jnp.where(slab + wedge > 0, 1, 2)
+    each_row(0, begun, all_tiles(first_pass))
     each_row(2, split, all_tiles(interior_one))
     pl.when(greeted > 0)(lambda: pl.semaphore_wait(barrier, greeted))
     for j in range(1, wedges):
@@ -440,7 +475,8 @@
     for side, jump in beside:
         pl.when(wedge + jump >= wedges)(first_phi[side].start)
     lax.fori_loop(
-        0, 3, lambda i, _: (all_tiles(edge_one)(jnp.where(i == 0, 1, rows - 3 + i)), 0)[1], 0
+        begun - 1, 3,
+        lambda i, _: (all_tiles(first_pass)(jnp.where(i == 0, 1, rows - 3 + i)), 0)[1], 0,
     )
 
     @pl.when(wedge + 1 < wedges)
@@ -452,6 +488,7 @@
     for side, jump in beside:
         pl.when(wedge + jump < wedges)(first_phi[side].start)
     each_row(split, rows - 2, all_tiles(interior_one))
+    each_row(rows - 2, rows - 1, all_tiles(lambda f, t: inner_face(first, f, t)))
     await_bytes(wedge_got.at[pl.ds(1, wedges - 1)], mass_recv.at[0])
     own = jnp.zeros((1, lanes), jnp.float32)
     for w in range(wedges):
@@ -462,21 +499,16 @@
     await_bytes(halo.at[pl.ds(0, 2)], phi_recv.at[0])
     for side in range(2):
         phi_unpack(first, 0, side, whole)
-    each_edge(all_tiles(lambda r, t: add_one(r, t, radial=False)))
-
-    def radial_side(step, copies, buffer, after, turn, send):
+    each_edge(all_tiles(phi_one))
+
+    def radial_side(step, copies, buffer, after, then=None):
         low = half == step
-        base = jnp.where(low, 0, rows - 2)
         for t in range(tiles):
             pl.when(low)(lambda: low_land(copies[t], buffer, t, after))
             pl.when(jnp.logical_not(low))(lambda: high_land(copies[t], buffer, t, after))
-            each_row(0, 2, lambda i: turn(base + i, t))
-            if send:
-                pl.when(low)(lambda: down_start(send[t]))
-                pl.when(jnp.logical_not(low))(lambda: up_start(send[t]))
-
-    def radial_one(r, t):
-        add_one(r, t, around_phi=False)
+            side_faces(buffer, low, t)
+            if then:
+                then(t)
 
     def row_of(i):
         return jnp.where(is_inner, i, rows - 1 - i)
@@ -537,25 +569,29 @@
         each_from(0, rows - 2, all_tiles(lambda r, t: gravity(r + 2, t)))
 
     slab_start(4, 6)
-    radial_side(0, first_radial, first, None, radial_one, None)
+    radial_side(0, first_radial, first, None)
     slab_start(6, slabs)
     passing_start(second_radial, first_radial, is_inner, range(tiles))
-    each_row(2, rows - 2, all_tiles(lambda r, t: add_one(r, t, radial=False)))
+    each_row(2, rows - 2, all_tiles(phi_one))
     phi_leave(main_phi, main)
-    passing_start(second_radial, first_radial, is_outer, range(1))
     ahead = jnp.where(is_inner, rows - 4, 0)
     pl.when(is_inner)(masses)
     each_from(0, ahead, all_tiles(theta_two))
-    radial_side(1, first_radial, first, None, radial_one, None)
-    passing_start(second_radial, first_radial, is_outer, range(1, tiles))
-    for t in range(tiles):
+
+    def second_start(t):
         pl.when(is_inner)(lambda: up_start(second_radial[t]))
         pl.when(is_outer)(lambda: down_start(second_radial[t]))
+        passing_start(second_radial, first_radial, is_outer, [t])
+
+    radial_side(
+        1, first_radial, first, None,
+        second_start,
+    )
     phi_leave(late_phi, late)
     pl.when(is_outer)(masses)
     each_from(rows - 2, rows, all_tiles(lambda r, t: gravity(r + 2, t)))
     each_from(ahead, rows, all_tiles(theta_two))
-    each_row(2, rows - 2, all_tiles(radial_two))
+    each_row(2, rows - 1, all_tiles(lambda f, t: inner_face(second, f, t)))
     phi_land(1, main)
     each_from(0, rows - 2, all_tiles(phi_two))
     phi_land(2, late)
@@ -567,8 +603,8 @@
         beyond = jnp.sum(below(line - rows) * slab_got[0], axis=1, keepdims=True)
         pull[...] = pull[...] + strength * beyond / (further * further)
 
-    radial_side(0, second_radial, second, gravity, radial_two, None)
-    radial_side(1, second_radial, second, gravity, radial_two, None)
+    radial_side(0, second_radial, second, gravity)
+    radial_side(1, second_radial, second, gravity)
 
     await_bytes(halo, phi_send.at[0])
     await_bytes(wedge_got.at[pl.ds(1, wedges - 1)], mass_send.at[0])

time: 18.3 us -> 18.2 us (level)
  Pallas kernels: 16.9 us -> 16.7 us
where the time goes in v5:
time: 18.2 us; the launch traced here: 18 us
  Pallas kernels  16.7 us (92%)
  between operations  1.28 us (7%)
    pallas_call x1, Pallas kernels, body(): pl.pallas_call(functools.partial(kernel, sizes, (slabs, wedges)), out_sha...  15.9 us
    pallas_call x1, Pallas kernels, body(): pl.pallas_call(store, out_shape=(jax.ShapeDtypeStruct(conserved.shape, jn...  0.81 us

profile of v5, /device:TPU:13, one launch (start us, length us, event | category | flops | bytes accessed | tf_op | source)
XLA Modules:
  0.0 18.0 jit_solution(2179518936103726435)
XLA Ops:
  1.3 15.9 %shard_map.50 = (f32[8,8,16,128]{3,2,1,0:T(8,128)S(1)}, f32[1,8]{1,0:T(1,128)S(1)}) custom-call(f32[1]{0:T(128)S(6)} %copy.5.core_ref, f32[8,128]{1,0:T(8,128)} %constant.2.clone.table_ref, f32[8,8,16,128]{3,2,1,0:T(8,128)} %input_ref.1), custom_call_target="tpu_custom_call" | custom-call | tf_op jit(solution)/shard_map/pallas_call | solution.py:648
  17.2 0.8 %shard_map.51 = (f32[8,8,16,128]{3,2,1,0:T(8,128)}, f32[8]{0:T(128)}) custom-call(f32[8,8,16,128]{3,2,1,0:T(8,128)S(1)} %get-tuple-element.4.advanced_ref, f32[8]{0:T(128)S(1)} %bitcast.1), custom_call_target="tpu_custom_call" | custom-call | tf_op jit(solution)/shard_map/pallas_call | solution.py:681

commit v6 on v5

--- a/solution.py
+++ b/solution.py
@@ -520,7 +520,6 @@
         for t in chosen:
             @pl.when(which)
             def _():
-                pl.when(is_inner & has_up)(gates[t][0].wait_send)
                 pl.when(is_outer & has_down)(gates[t][1].wait_send)
                 pl.when(is_inner)(lambda: down_start(copies[t]))
                 pl.when(is_outer)(lambda: up_start(copies[t]))
@@ -574,7 +573,7 @@
     passing_start(second_radial, first_radial, is_inner, range(tiles))
     each_row(2, rows - 2, all_tiles(phi_one))
     phi_leave(main_phi, main)
-    ahead = jnp.where(is_inner, rows - 4, 0)
+    ahead = jnp.where(is_inner, rows - 3, 0)
     pl.when(is_inner)(masses)
     each_from(0, ahead, all_tiles(theta_two))
 
@@ -614,7 +613,7 @@
             await_bytes(slab_got.at[pl.ds(0, slabs - 1 - j + min(j, 1))], mass_send.at[1])
 
     for up, down in first_radial:
-        pl.when(has_up & is_outer)(up.wait_send)
+        pl.when(has_up)(up.wait_send)
         pl.when(has_down & is_inner)(down.wait_send)
     def second_sent(sides):
         moved = second.at[:, pl.ds(0, 2 * sides), pl.ds(PAD, cells), :]

time: 18.2 us -> 18.1 us (level)
  no operation moved by 1% of the time
where the time goes in v6:
time: 18.1 us; the launch traced here: 18 us
  Pallas kernels  16.7 us (92%)
  between operations  1.28 us (7%)
    pallas_call x1, Pallas kernels, body(): pl.pallas_call(functools.partial(kernel, sizes, (slabs, wedges)), out_sha...  15.9 us
    pallas_call x1, Pallas kernels, body(): pl.pallas_call(store, out_shape=(jax.ShapeDtypeStruct(conserved.shape, jn...  0.81 us

profile of v6, /device:TPU:13, one launch (start us, length us, event | category | flops | bytes accessed | tf_op | source)
XLA Modules:
  0.0 18.0 jit_solution(14750967925415598702)
XLA Ops:
  1.3 15.9 %shard_map.50 = (f32[8,8,16,128]{3,2,1,0:T(8,128)S(1)}, f32[1,8]{1,0:T(1,128)S(1)}) custom-call(f32[1]{0:T(128)S(6)} %copy.5.core_ref, f32[8,128]{1,0:T(8,128)} %constant.2.clone.table_ref, f32[8,8,16,128]{3,2,1,0:T(8,128)} %input_ref.1), custom_call_target="tpu_custom_call" | custom-call | tf_op jit(solution)/shard_map/pallas_call | solution.py:647
  17.2 0.8 %shard_map.51 = (f32[8,8,16,128]{3,2,1,0:T(8,128)}, f32[8]{0:T(128)}) custom-call(f32[8,8,16,128]{3,2,1,0:T(8,128)S(1)} %get-tuple-element.4.advanced_ref, f32[8]{0:T(128)S(1)} %bitcast.1), custom_call_target="tpu_custom_call" | custom-call | tf_op jit(solution)/shard_map/pallas_call | solution.py:680

commit v7 on v6

--- a/solution.py
+++ b/solution.py
@@ -475,7 +475,7 @@
     for side, jump in beside:
         pl.when(wedge + jump >= wedges)(first_phi[side].start)
     lax.fori_loop(
-        begun - 1, 3,
+        begun - 1, 2,
         lambda i, _: (all_tiles(first_pass)(jnp.where(i == 0, 1, rows - 3 + i)), 0)[1], 0,
     )
 
@@ -487,6 +487,7 @@
         pl.when(wedge + j < wedges)(wedge_copies[j - 1].start)
     for side, jump in beside:
         pl.when(wedge + jump < wedges)(first_phi[side].start)
+    each_row(rows - 1, rows, all_tiles(first_pass))
     each_row(split, rows - 2, all_tiles(interior_one))
     each_row(rows - 2, rows - 1, all_tiles(lambda f, t: inner_face(first, f, t)))
     await_bytes(wedge_got.at[pl.ds(1, wedges - 1)], mass_recv.at[0])

time: 18.1 us -> 18.2 us (level)
  no operation moved by 1% of the time
where the time goes in v7:
time: 18.2 us; the launch traced here: 18 us
  Pallas kernels  16.7 us (92%)
  between operations  1.28 us (7%)
    pallas_call x1, Pallas kernels, body(): pl.pallas_call(functools.partial(kernel, sizes, (slabs, wedges)), out_sha...  15.9 us
    pallas_call x1, Pallas kernels, body(): pl.pallas_call(store, out_shape=(jax.ShapeDtypeStruct(conserved.shape, jn...  0.81 us

profile of v7, /device:TPU:13, one launch (start us, length us, event | category | flops | bytes accessed | tf_op | source)
XLA Modules:
  0.0 18.0 jit_solution(12439324003581484391)
XLA Ops:
  1.3 15.9 %shard_map.50 = (f32[8,8,16,128]{3,2,1,0:T(8,128)S(1)}, f32[1,8]{1,0:T(1,128)S(1)}) custom-call(f32[1]{0:T(128)S(6)} %copy.5.core_ref, f32[8,128]{1,0:T(8,128)} %constant.2.clone.table_ref, f32[8,8,16,128]{3,2,1,0:T(8,128)} %input_ref.1), custom_call_target="tpu_custom_call" | custom-call | tf_op jit(solution)/shard_map/pallas_call | solution.py:648
  17.2 0.8 %shard_map.51 = (f32[8,8,16,128]{3,2,1,0:T(8,128)}, f32[8]{0:T(128)}) custom-call(f32[8,8,16,128]{3,2,1,0:T(8,128)S(1)} %get-tuple-element.4.advanced_ref, f32[8]{0:T(128)S(1)} %bitcast.1), custom_call_target="tpu_custom_call" | custom-call | tf_op jit(solution)/shard_map/pallas_call | solution.py:681
